TPU v7x, 32 devices: a whole 2x2x4 slice. The times are simulated.
32 devices in a mesh: dp: 4 (over z), rows: 8 (over y, x, core).
Axes of the slice: x: 2, y: 2, z: 4, core: 2. Of those that a mesh axis runs over, the one named last changes fastest.
Arguments:
- owners: int32 [32768, 1], P(('dp', 'rows')), may hold values from 0 to 31; in each aligned block of 1024 rows (0 to 1023, 1024 to 2047, ...) at most 128 rows name the same one
- offsets: int32 [32768], P(('dp', 'rows')), may hold values from 0 to 8191
- gradients: bfloat16 [32768, 128], P(('dp', 'rows')), may hold values from -6 to 6
- embedding: float32 [262144, 128], P(('dp', 'rows')), may hold values from -6 to 6
- adagrad_state: float32 [262144], P(('dp', 'rows')), may hold values from 0.05 to 2
- next_owners: int32 [32768, 1], P(('dp', 'rows')), may hold values from 0 to 31; in each aligned block of 1024 rows (0 to 1023, 1024 to 2047, ...) at most 128 rows name the same one
- next_offsets: int32 [32768], P(('dp', 'rows')), may hold values from 0 to 8191
Outputs:
- new_embedding: float32 [262144, 128], P(('dp', 'rows'))
- new_state: float32 [262144], P(('dp', 'rows'))
- next_rows: bfloat16 [32768, 128], P(('dp', 'rows'))
Inputs may be any that keep to these rules, and one draw needn't show every extreme that they name: `owners`: within the 1024 rows of one device, at most 128 rows name the same block. `next_owners`: within the 1024 rows of one device, at most 128 rows name the same block.
All inputs are finite; a program needn't handle non-finite values.
Results may differ from a plain program's by a relative error of at most 0.0013.
Values may be sent and summed in bfloat16 or wider, within the bound.
A program may use at most 64 MiB of HBM per device.

v0:
```python
import jax
import jax.numpy as jnp
from jax import lax
from jax.experimental import pallas as pl
from jax.experimental.pallas import tpu as pltpu
from jax.sharding import PartitionSpec as P

BANKS = 4
LANES = 128
BASE = 256


def positions_of(owner_ids, next_ids, devices):
    lookups = owner_ids.shape[0]
    names = jnp.arange(devices, dtype=jnp.int32)[None, :]
    one_hot = jnp.concatenate(
        [owner_ids[:, None] == names, next_ids[:, None] == names], axis=1
    ).astype(jnp.bfloat16)
    index = jnp.arange(lookups, dtype=jnp.int32)
    earlier = (index[:, None] > index[None, :]).astype(jnp.bfloat16)
    ahead = jnp.dot(earlier, one_hot, preferred_element_type=jnp.float32)
    hits = ahead * one_hot.astype(jnp.float32)
    slots = jnp.sum(hits[:, :devices], axis=1), jnp.sum(hits[:, devices:], axis=1)
    return tuple(part.astype(jnp.int32) for part in slots)


def slot_table(owner_ids, slot_ids, offsets, devices, capacity):
    names = jnp.arange(devices, dtype=jnp.int32)[None, :]
    one_hot = (owner_ids[:, None] == names).astype(jnp.bfloat16)
    in_slot = slot_ids[:, None] == jnp.arange(capacity, dtype=jnp.int32)[None, :]
    high = (offsets // BASE).astype(jnp.float32)[:, None]
    low = (offsets % BASE).astype(jnp.float32)[:, None]
    columns = jnp.concatenate(
        [jnp.where(in_slot, high, 0.0), jnp.where(in_slot, low, 0.0), jnp.where(in_slot, 1.0, 0.0)],
        axis=1,
    ).astype(jnp.bfloat16)
    table = lax.dot_general(
        one_hot, columns, (((0,), (0,)), ((), ())), preferred_element_type=jnp.float32
    )
    return jnp.split(table, 3, axis=1)


def update_kernel(
    rows_hbm, wanted_hbm, incoming_ref, embedding_ref, state_ref,
    new_embedding_ref, new_state_ref, fetched_ref,
    *scratch,
):
    banks = scratch[:BANKS]
    table, picked, rows_ref, wanted_ref, in_sem, rows_sem, wanted_sem, out_sems = scratch[BANKS:]
    owned = table.shape[0]
    slots = picked.shape[0]
    blocks = incoming_ref.shape[0]
    capacity = slots // blocks
    chunks = out_sems.shape[0]
    chunk = owned // chunks

    rows_load = pltpu.make_async_copy(rows_hbm, rows_ref, rows_sem)
    rows_load.start()
    wanted_load = pltpu.make_async_copy(wanted_hbm, wanted_ref, wanted_sem)
    wanted_load.start()
    load = pltpu.make_async_copy(embedding_ref, table, in_sem)
    load.start()

    zero_rows = 128

    @pl.loop(0, owned // zero_rows)
    def _(step):
        for bank in banks:
            bank[pl.ds(pl.multiple_of(step * zero_rows, zero_rows), zero_rows), :] = jnp.zeros(
                (zero_rows, LANES), jnp.float32
            )

    group = next(size for size in (64, 32, 8) if capacity % size == 0)
    per_block = capacity // group
    rows_load.wait()

    @pl.loop(0, blocks * per_block)
    def _(step):
        start = pl.multiple_of(step * group, group)
        within = pl.multiple_of(lax.rem(step, per_block) * group, group)
        block = incoming_ref[lax.div(step, per_block), pl.ds(within, group), :].astype(jnp.float32)
        for first in range(0, group, BANKS):
            where = [rows_ref[start + first + k] for k in range(BANKS)]
            sums = [
                banks[k][pl.ds(where[k], 1), :] + block[first + k : first + k + 1, :]
                for k in range(BANKS)
            ]
            for k in range(BANKS):
                banks[k][pl.ds(where[k], 1), :] = sums[k]

    load.wait()
    for piece in range(chunks):

        @pl.loop(0, chunk // LANES, unroll=4)
        def _(step):
            tile = piece * (chunk // LANES) + step
            span = pl.ds(pl.multiple_of(tile * LANES, LANES), LANES)
            grad_sum = banks[0][span, :]
            for bank in banks[1:]:
                grad_sum = grad_sum + bank[span, :]
            mean = jnp.sum(grad_sum * grad_sum, axis=1, keepdims=True) * (1.0 / LANES)
            old = jnp.broadcast_to(state_ref[pl.ds(tile, 1), :], (LANES, LANES)).T
            state = old + mean
            new_state_ref[pl.ds(tile, 1), :] = state.T[0:1, :]
            table[span, :] = table[span, :] - 0.5 * grad_sum * lax.rsqrt(state)

        span = pl.ds(piece * chunk, chunk)
        pltpu.make_async_copy(
            table.at[span, :], new_embedding_ref.at[span, :], out_sems.at[piece]
        ).start()

    wanted_load.wait()

    @pl.loop(0, slots // group)
    def _(step):
        start = pl.multiple_of(step * group, group)
        for k in range(group):
            picked[pl.ds(start + k, 1), :] = table[pl.ds(wanted_ref[start + k], 1), :]

    @pl.loop(0, slots // LANES)
    def _(step):
        span = pl.ds(pl.multiple_of(step * LANES, LANES), LANES)
        fetched_ref[span, :] = picked[span, :].astype(jnp.bfloat16)

    for piece in range(chunks):
        span = pl.ds(piece * chunk, chunk)
        pltpu.make_async_copy(
            table.at[span, :], new_embedding_ref.at[span, :], out_sems.at[piece]
        ).wait()


def update(rows, wanted, incoming, embedding, state):
    owned, columns = embedding.shape
    slots = rows.shape[0]
    chunks = 8
    vmem = pl.BlockSpec(memory_space=pltpu.VMEM)
    hbm = pl.BlockSpec(memory_space=pltpu.HBM)
    new_embedding, new_state, fetched = pl.pallas_call(
        update_kernel,
        name="update",
        out_shape=(
            jax.ShapeDtypeStruct((owned, columns), jnp.float32),
            jax.ShapeDtypeStruct((owned // LANES, LANES), jnp.float32),
            jax.ShapeDtypeStruct((slots, columns), jnp.bfloat16),
        ),
        in_specs=[hbm, hbm, vmem, hbm, vmem],
        out_specs=(hbm, vmem, vmem),
        scratch_shapes=[pltpu.VMEM((owned + 8, columns), jnp.float32)] * BANKS
        + [
            pltpu.VMEM((owned, columns), jnp.float32),
            pltpu.VMEM((slots, columns), jnp.float32),
            pltpu.SMEM((slots,), jnp.int32),
            pltpu.SMEM((slots,), jnp.int32),
            pltpu.SemaphoreType.DMA,
            pltpu.SemaphoreType.DMA,
            pltpu.SemaphoreType.DMA,
            pltpu.SemaphoreType.DMA((chunks,)),
        ],
        compiler_params=pltpu.CompilerParams(vmem_limit_bytes=50 * 1024 * 1024),
    )(rows, wanted, incoming, embedding, state.reshape(owned // LANES, LANES))
    return new_embedding, new_state.reshape(owned), fetched


def on_device(owners, offsets, gradients, embedding, adagrad_state, next_owners, next_offsets):
    axes = ("dp", "rows")
    devices = lax.axis_size(axes)
    lookups, columns = gradients.shape
    owned_rows = embedding.shape[0]
    capacity = max(2, 4 * lookups // devices)
    slots = devices * capacity
    owner_ids, next_ids = owners[:, 0], next_owners[:, 0]
    slot_ids, next_slots = positions_of(owner_ids, next_ids, devices)
    places = owner_ids * capacity + slot_ids
    next_places = next_ids * capacity + next_slots
    high, low, used = slot_table(owner_ids, slot_ids, offsets, devices, capacity)
    next_high, next_low, _ = slot_table(next_ids, next_slots, next_offsets, devices, capacity)
    high = jnp.where(used > 0, high, owned_rows // BASE)
    ids = jnp.concatenate([high, low, next_high, next_low], axis=1).astype(jnp.bfloat16)
    id_rows = 8 * -(-4 * capacity // (8 * columns))
    ids = jnp.pad(ids, ((0, 0), (0, id_rows * columns - 4 * capacity)))
    slot_index = jnp.arange(slots, dtype=jnp.int32)
    outgoing = jnp.dot(
        (slot_index[:, None] == places[None, :]).astype(jnp.bfloat16),
        gradients,
        preferred_element_type=jnp.float32,
    ).astype(jnp.bfloat16)
    outgoing = jnp.concatenate(
        [outgoing.reshape(devices, capacity, columns), ids.reshape(devices, id_rows, columns)], axis=1
    )
    incoming = lax.all_to_all(outgoing, axes, split_axis=0, concat_axis=0, tiled=True)
    ids = incoming[:, capacity:].reshape(devices, id_rows * columns)[:, : 4 * capacity]
    ids = ids.astype(jnp.int32).reshape(devices, 4, capacity)
    rows = (ids[:, 0] * BASE + ids[:, 1]).reshape(-1)
    wanted = (ids[:, 2] * BASE + ids[:, 3]).reshape(-1)
    new_embedding, new_state, fetched = update(rows, wanted, incoming, embedding, adagrad_state)
    returned = lax.all_to_all(
        fetched.reshape(devices, capacity, columns), axes, split_axis=0, concat_axis=0, tiled=True
    )
    next_rows = jnp.dot(
        (next_places[:, None] == slot_index[None, :]).astype(jnp.bfloat16),
        returned.reshape(slots, columns),
        preferred_element_type=jnp.float32,
    ).astype(jnp.bfloat16)
    return (new_embedding, new_state, next_rows)


def solution(mesh):
    in_specs = (
        P(("dp", "rows"), None),
        P(("dp", "rows")),
        P(("dp", "rows"), None),
        P(("dp", "rows"), None),
        P(("dp", "rows")),
        P(("dp", "rows"), None),
        P(("dp", "rows")),
    )
    out_specs = (P(("dp", "rows"), None), P(("dp", "rows")), P(("dp", "rows"), None))
    return jax.shard_map(
        on_device, mesh=mesh, in_specs=in_specs, out_specs=out_specs, check_vma=False
    )
```

profile of v0, /device:TPU:0, one launch (start us, length us, event | category | flops | bytes accessed | tf_op | source)
XLA Modules:
  0.0 94.4 jit_solution(10140560453087424178)
XLA Ops:
  0.6 0.0 copy-start
  0.6 0.0 copy-start.2
  0.7 0.0 copy-start.4
  0.7 0.8 iota_compare_fusion.15
  1.5 0.0 copy-start.5
  1.5 0.6 fusion.7
  2.1 0.0 copy-start.3
  2.1 0.0 copy-done.2
  2.1 0.0 copy-done.4
  2.2 0.2 select_convert_fusion.3
  2.4 0.5 select_convert_fusion.5
  2.9 0.2 fusion.8
  3.1 0.0 copy-done.5
  3.2 0.2 select_convert_fusion
  3.4 0.5 select_convert_fusion.2
  3.8 0.0 copy-done.3
  3.8 0.2 fusion.14
  4.1 0.0 copy-done
  4.1 2.9 %fusion.4 = bf16[4096,128]{1,0:T(8,128)(2,1)S(1)} fusion(bf16[1024,128]{1,0:T(8,128)(2,1)S(1)} %copy-done, s32[1024]{0:T(1024)S(1)} %multiply_add_fusion.1), kind=kOutput, calls=%fused_computation.6 | convolution fusion | flops 1078460416 | bytes 1314816 | tf_op jit(solution)/shard_map/dot_general | solution.py:182
  7.1 0.0 copy-start.1
  7.1 0.1 pad_maximum_fusion
  7.2 36.5 %all_to_all.10.incoming_ref = bf16[32,136,128]{2,1,0:T(8,128)(2,1)S(1)} all-to-all(bf16[32,136,128]{2,1,0:T(8,128)(2,1)S(1)} %pad_maximum_fusion), channel_id=1, replica_groups=mesh['dp'=4,'rows'=8] {'dp','rows'}, dimensions={0} | all-to-all | bytes 2228224 | tf_op jit(solution)/shard_map/all_to_all | solution.py:190
  43.8 0.0 copy-done.1
  43.8 18.2 %update.1 = (f32[8192,128]{1,0:T(8,128)}, f32[64,128]{1,0:T(8,128)}, bf16[4096,128]{1,0:T(8,128)(2,1)}) custom-call(s32[4096]{0:T(1024)S(1)} %bitcast.21, s32[4096]{0:T(1024)S(1)} %bitcast.20, bf16[32,136,128]{2,1,0:T(8,128)(2,1)S(1)} %all_to_all.10.incoming_ref, f32[8192,128]{1,0:T(8,128)} %embedding_ref.1, f32[64,128]{1,0:T(8,128)S(1)} %bitcast.22), custom_call_target="tpu_custom_call" | custom-call | tf_op jit(solution)/shard_map/update/pallas_call | solution.py:138
  62.1 2.7 %all-to-all-start.1 = ((bf16[32,128,128]{2,1,0:T(8,128)(2,1)}), bf16[32,128,128]{2,1,0:T(8,128)(2,1)S(1)}, u32[]{:S(2)}, u32[]{:S(2)}) async-start(bf16[32,128,128]{2,1,0:T(8,128)(2,1)} %bitcast.9), calls=%async_computation.1 | async-start | bytes 2097152 | tf_op jit(solution)/shard_map/all_to_all | solution.py:196
  64.7 26.2 %all-to-all-done.1 = bf16[32,128,128]{2,1,0:T(8,128)(2,1)S(1)} async-done(((bf16[32,128,128]{2,1,0:T(8,128)(2,1)}), bf16[32,128,128]{2,1,0:T(8,128)(2,1)S(1)}, u32[]{:S(2)}, u32[]{:S(2)}) %all-to-all-start.1) | async-done | bytes 1048608 | tf_op jit(solution)/shard_map/all_to_all | solution.py:196
  90.9 3.5 %fusion.6 = bf16[1024,128]{1,0:T(8,128)(2,1)} fusion(bf16[4096,128]{1,0:T(8,128)(2,1)S(1)} %bitcast.23, s32[1024]{0:T(1024)S(1)} %bitcast.34), kind=kOutput, calls=%fused_computation.9 | convolution fusion | flops 1078067200 | bytes 1314816 | tf_op jit(solution)/shard_map/dot_general | solution.py:199
  (17 shorter events, 0.2 us)
Async XLA Ops:
  0.6 3.5 %copy-start = (bf16[1024,128]{1,0:T(8,128)(2,1)S(1)}, bf16[1024,128]{1,0:T(8,128)(2,1)}, u32[]{:S(2)}) copy-start(bf16[1024,128]{1,0:T(8,128)(2,1)} %param.9) | copy-start | bytes 786436
  0.6 1.5 %copy-start.2 = (s32[1024,1]{0,1:T(1,128)S(1)}, s32[1024,1]{0,1:T(1,128)}, u32[]{:S(2)}) copy-start(s32[1024,1]{0,1:T(1,128)} %param.7) | copy-start | bytes 12292
  0.7 1.5 %copy-start.4 = (s32[1024]{0:T(1024)S(1)}, s32[1024]{0:T(1024)}, u32[]{:S(2)}) copy-start(s32[1024]{0:T(1024)} %param.8) | copy-start | bytes 12292
  1.5 1.7 %copy-start.5 = (s32[1024]{0:T(1024)S(1)}, s32[1024]{0:T(1024)}, u32[]{:S(2)}) copy-start(s32[1024]{0:T(1024)} %param.13) | copy-start | bytes 12292
  2.1 1.8 %copy-start.3 = (s32[1024,1]{0,1:T(1,128)S(1)}, s32[1024,1]{0,1:T(1,128)}, u32[]{:S(2)}) copy-start(s32[1024,1]{0,1:T(1,128)} %param.12) | copy-start | bytes 12292
  7.1 36.7 %copy-start.1 = (f32[8192]{0:T(1024)S(1)}, f32[8192]{0:T(1024)}, u32[]{:S(2)}) copy-start(f32[8192]{0:T(1024)} %param.11) | copy-start | bytes 98308
  62.1 28.9 %all-to-all-start.1 = ((bf16[32,128,128]{2,1,0:T(8,128)(2,1)}), bf16[32,128,128]{2,1,0:T(8,128)(2,1)S(1)}, u32[]{:S(2)}, u32[]{:S(2)}) async-start(bf16[32,128,128]{2,1,0:T(8,128)(2,1)} %bitcast.9), calls=%async_computation.1 | async-start | bytes 2097152 | tf_op jit(solution)/shard_map/all_to_all | solution.py:196
where the time goes:
time: 94.8 us; the launch traced here: 94.4 us
  blocking collectives  36.5 us (39%)
  waiting for transfers between devices  26.2 us (28%)
  Pallas kernels  18.2 us (19%)
  matrix products  7.5 us (8%)
  starting transfers between devices  2.66 us (3%)
  other arithmetic  2.37 us (2%)
    all_to_all x1, blocking collectives, on_device(): lax.all_to_all(outgoing, axes, split_axis=0, concat_axis=0, tiled=True)  36.5 us
    all_to_all x1, waiting for transfers between devices, on_device(): lax.all_to_all(fetched.reshape(devices, capacity, columns), axes, split_a...  26.2 us
    pallas_call x1, Pallas kernels, update(): pl.pallas_call(update_kernel, name='update', out_shape=(jax.ShapeDtypeStr...  18.2 us
    dot_general x1, matrix products, on_device(): jnp.dot((next_places[:, None] == slot_index[None, :]).astype(jnp.bfloat16...  3.51 us
    dot_general x1, matrix products, on_device(): jnp.dot((slot_index[:, None] == places[None, :]).astype(jnp.bfloat16), gr...  2.95 us
    all_to_all x1, starting transfers between devices, on_device(): lax.all_to_all(fetched.reshape(devices, capacity, columns), axes, split_a...  2.66 us
  transfers between devices with their start and end apart: 1, of which 1 were waited for; matrix products, arithmetic and copies ran while one was open for 0% of the time, Pallas kernels for 0%

commit v1 on v0

v1 whole, which is shorter than its diff:
```python
import functools

import jax
import jax.numpy as jnp
from jax import lax
from jax.experimental import pallas as pl
from jax.experimental.pallas import tpu as pltpu
from jax.sharding import PartitionSpec as P

LANES = 128
SUB = 16
BASE = 256
MESH = pl.DeviceIdType.MESH


def positions_of(owner_ids, next_ids, devices):
    lookups = owner_ids.shape[0]
    names = jnp.arange(devices, dtype=jnp.int32)[None, :]
    one_hot = jnp.concatenate(
        [owner_ids[:, None] == names, next_ids[:, None] == names], axis=1
    ).astype(jnp.bfloat16)
    index = jnp.arange(lookups, dtype=jnp.int32)
    earlier = (index[:, None] > index[None, :]).astype(jnp.bfloat16)
    ahead = jnp.dot(earlier, one_hot, preferred_element_type=jnp.float32)
    hits = ahead * one_hot.astype(jnp.float32)
    slots = jnp.sum(hits[:, :devices], axis=1), jnp.sum(hits[:, devices:], axis=1)
    return tuple(part.astype(jnp.int32) for part in slots)


def slot_table(owner_ids, slot_ids, values, devices, capacity):
    names = jnp.arange(devices, dtype=jnp.int32)[None, :]
    one_hot = (owner_ids[:, None] == names).astype(jnp.bfloat16)
    in_slot = slot_ids[:, None] == jnp.arange(capacity, dtype=jnp.int32)[None, :]
    columns = jnp.concatenate(
        [jnp.where(in_slot, value.astype(jnp.float32)[:, None], 0.0) for value in values],
        axis=1,
    ).astype(jnp.bfloat16)
    table = lax.dot_general(
        one_hot, columns, (((0,), (0,)), ((), ())), preferred_element_type=jnp.float32
    )
    return table.reshape(devices, len(values), capacity)


def plane_order(dp):
    middle = dp // 2
    return [middle] + [d for d in range(1, dp) if d != middle] + [0]


def peer(dp, rows, dz, dr, sign):
    z, r = lax.axis_index("dp"), lax.axis_index("rows")
    if sign > 0:
        return (lax.rem(z + dz, dp), lax.rem(r + dr, rows))
    return (lax.rem(z + dp - dz, dp), lax.rem(r + rows - dr, rows))


def greet(dp, rows):
    barrier = pltpu.get_barrier_semaphore()

    @pl.loop(1, dp * rows)
    def _(i):
        pl.semaphore_signal(
            barrier,
            inc=1,
            device_id=peer(dp, rows, lax.div(i, rows), lax.rem(i, rows), 1),
            device_id_type=MESH,
        )


def gathered(dp, rows):
    pl.semaphore_wait(pltpu.get_barrier_semaphore(), dp * rows - 1)


def send_kernel(
    dp, rows,
    place_ref, gradients_ref, meta_ref,
    acc_ref, met_ref,
    outgoing, incoming, meta_send, meta_recv, data_send, data_recv,
):
    devices = dp * rows
    slots = outgoing.shape[0]
    capacity = slots // devices
    columns = gradients_ref.shape[1]
    half = acc_ref.shape[0]
    group = 2 if capacity == LANES else 1
    depth = group * capacity

    greet(dp, rows)

    made = 512
    place = place_ref[...]
    lookups = place.shape[1]

    @pl.loop(0, slots // made)
    def _(step):
        start = pl.multiple_of(step * made, made)
        names = lax.broadcasted_iota(jnp.int32, (made, lookups), 0) + start
        chosen = jnp.where(names == place, 1.0, 0.0).astype(jnp.bfloat16)
        outgoing[pl.ds(start, made), :] = jnp.dot(
            chosen, gradients_ref[...], preferred_element_type=jnp.float32
        ).astype(jnp.bfloat16)

    @pl.loop(0, half // LANES)
    def _(step):
        acc_ref[pl.ds(pl.multiple_of(step * LANES, LANES), LANES), :] = jnp.zeros(
            (LANES, acc_ref.shape[1]), jnp.float32
        )

    gathered(dp, rows)

    def copies(dz, dr, sign):
        i = dz * rows + dr
        span = pl.ds(pl.multiple_of(i * capacity, capacity), capacity)
        to = peer(dp, rows, dz, dr, sign)
        meta = pltpu.make_async_remote_copy(
            src_ref=meta_ref.at[i], dst_ref=met_ref.at[i],
            send_sem=meta_send.at[i], recv_sem=meta_recv.at[i],
            device_id=to, device_id_type=MESH,
        )
        data = pltpu.make_async_remote_copy(
            src_ref=outgoing.at[span, :], dst_ref=incoming.at[span, :],
            send_sem=data_send.at[i], recv_sem=data_recv.at[i],
            device_id=to, device_id_type=MESH,
        )
        return meta, data

    for dz in plane_order(dp):

        @pl.loop(0 if dz else 1, rows)
        def _(dr):
            meta, data = copies(dz, dr, 1)
            meta.start()
            data.start()

    met_ref[0] = meta_ref[0]
    incoming[0:capacity, :] = outgoing[0:capacity, :]

    chunk = min(1024, half)
    names = chunk // SUB

    def accumulate(tile):
        met = [met_ref[tile * group + k].astype(jnp.float32) for k in range(group)]
        high = jnp.concatenate([m[0:1, :] for m in met], axis=1)
        both = jnp.concatenate([m[1:2, :] for m in met], axis=1)
        low = jnp.where(both >= SUB, both - SUB, both)
        ones = jnp.where(
            lax.broadcasted_iota(jnp.int32, (SUB, depth), 0).astype(jnp.float32) == low, 1.0, 0.0
        ).astype(jnp.bfloat16)
        parts = []
        for k in range(group):
            upper = jnp.broadcast_to(met[k][1:2, :], (columns, capacity)).T >= SUB
            start = pl.multiple_of((tile * group + k) * capacity, capacity)
            block = incoming[pl.ds(start, capacity), :].astype(jnp.float32)
            parts.append(
                jnp.concatenate(
                    [jnp.where(upper, 0.0, block), jnp.where(upper, block, 0.0)], axis=1
                ).astype(jnp.bfloat16)
            )
        wide = jnp.concatenate(parts, axis=0) if group > 1 else parts[0]
        high = jnp.broadcast_to(high, (SUB, depth))

        @pl.loop(0, half // chunk)
        def _(step):
            shifted = (high - (step * names).astype(jnp.float32)).astype(jnp.bfloat16)
            zero = jnp.zeros((SUB, depth), jnp.bfloat16)
            chosen = jnp.concatenate(
                [jnp.where(shifted == jnp.bfloat16(name), ones, zero) for name in range(names)], axis=0
            )
            span = pl.ds(pl.multiple_of(step * chunk, chunk), chunk)
            acc_ref[span, :] += jnp.dot(chosen, wide, preferred_element_type=jnp.float32)

    per_plane = rows // group
    for dz in plane_order(dp):

        @pl.loop(0, per_plane)
        def _(step):
            for k in range(group):
                dr = step * group + k

                def arrive():
                    meta, data = copies(dz, dr, -1)
                    meta.wait_recv()
                    data.wait_recv()

                if dz == 0:
                    pl.when(dr > 0)(arrive)
                else:
                    arrive()
            accumulate(dz * per_plane + step)

    for dz in plane_order(dp):

        @pl.loop(0 if dz else 1, rows)
        def _(dr):
            meta, data = copies(dz, dr, 1)
            meta.wait_send()
            data.wait_send()


def send_gradients(dp, rows, place, gradients, meta, owned):
    devices, _, capacity = meta.shape
    slots = devices * capacity
    columns = gradients.shape[1]
    vmem = pl.BlockSpec(memory_space=pltpu.VMEM)
    return pl.pallas_call(
        functools.partial(send_kernel, dp, rows),
        name="send_gradients",
        out_shape=(
            jax.ShapeDtypeStruct((owned // 2, 2 * columns), jnp.float32),
            jax.ShapeDtypeStruct(meta.shape, meta.dtype),
        ),
        in_specs=[vmem] * 3,
        out_specs=(vmem, vmem),
        scratch_shapes=[
            pltpu.VMEM((slots, columns), jnp.bfloat16),
            pltpu.VMEM((slots, columns), jnp.bfloat16),
        ]
        + [pltpu.SemaphoreType.DMA((devices,))] * 4,
        compiler_params=pltpu.CompilerParams(
            collective_id=0, has_side_effects=True, vmem_limit_bytes=32 * 1024 * 1024
        ),
    )(place.reshape(1, -1), gradients, meta)


def update_kernel(
    acc_ref, embedding_ref, state_ref, new_embedding_ref, new_state_ref, table, in_sems, out_sems
):
    owned = table.shape[0]
    half = acc_ref.shape[0]
    chunks = in_sems.shape[0]
    chunk = owned // chunks

    def load(piece):
        span = pl.ds(piece * chunk, chunk)
        return pltpu.make_async_copy(embedding_ref.at[span, :], table.at[span, :], in_sems.at[piece])

    def store(piece):
        span = pl.ds(piece * chunk, chunk)
        return pltpu.make_async_copy(
            table.at[span, :], new_embedding_ref.at[span, :], out_sems.at[piece]
        )

    for piece in range(chunks):
        load(piece).start()
    for piece in range(chunks):
        load(piece).wait()
        side = piece * chunk // half

        @pl.loop(0, chunk // LANES, unroll=4)
        def _(step):
            tile = piece * (chunk // LANES) + step
            span = pl.ds(pl.multiple_of(tile * LANES, LANES), LANES)
            low = pl.ds(pl.multiple_of(tile * LANES - side * half, LANES), LANES)
            grad_sum = acc_ref[low, side * LANES : (side + 1) * LANES]
            mean = jnp.sum(grad_sum * grad_sum, axis=1, keepdims=True) * (1.0 / LANES)
            old = jnp.broadcast_to(state_ref[pl.ds(tile, 1), :], (LANES, LANES)).T
            state = old + mean
            new_state_ref[pl.ds(tile, 1), :] = state.T[0:1, :]
            table[span, :] = table[span, :] - 0.5 * grad_sum * lax.rsqrt(state)

        store(piece).start()
    for piece in range(chunks):
        store(piece).wait()


def update(acc, embedding, state):
    owned, columns = embedding.shape
    chunks = 8
    vmem = pl.BlockSpec(memory_space=pltpu.VMEM)
    hbm = pl.BlockSpec(memory_space=pltpu.HBM)
    new_embedding, new_state, table = pl.pallas_call(
        update_kernel,
        name="update",
        out_shape=(
            jax.ShapeDtypeStruct((owned, columns), jnp.float32),
            jax.ShapeDtypeStruct((owned // LANES, LANES), jnp.float32),
            jax.ShapeDtypeStruct((owned, columns), jnp.float32),
        ),
        in_specs=[vmem, hbm, vmem],
        out_specs=(hbm, vmem, vmem),
        scratch_shapes=[
            pltpu.SemaphoreType.DMA((chunks,)),
            pltpu.SemaphoreType.DMA((chunks,)),
        ],
        compiler_params=pltpu.CompilerParams(vmem_limit_bytes=32 * 1024 * 1024),
    )(acc, embedding, state.reshape(owned // LANES, LANES))
    return new_embedding, new_state.reshape(owned), table


def fetch_kernel(
    dp, rows,
    wanted_hbm, place_ref, table_ref, next_ref,
    wanted_ref, picked, outgoing, incoming, total, wanted_sem, data_send, data_recv,
):
    devices = dp * rows
    slots = outgoing.shape[0]
    capacity = slots // devices
    group = 2 if capacity == LANES else 1
    depth = group * capacity

    greet(dp, rows)
    load = pltpu.make_async_copy(wanted_hbm, wanted_ref, wanted_sem)
    load.start()
    total[...] = jnp.zeros(total.shape, jnp.float32)
    load.wait()

    def copy(dz, dr, sign):
        i = dz * rows + dr
        span = pl.ds(pl.multiple_of(i * capacity, capacity), capacity)
        return pltpu.make_async_remote_copy(
            src_ref=outgoing.at[span, :], dst_ref=incoming.at[span, :],
            send_sem=data_send.at[i], recv_sem=data_recv.at[i],
            device_id=peer(dp, rows, dz, dr, sign), device_id_type=MESH,
        )

    def gather(i):
        start = pl.multiple_of(i * capacity, capacity)
        for k in range(capacity):
            picked[pl.ds(k, 1), :] = table_ref[pl.ds(wanted_ref[start + k], 1), :]
        outgoing[pl.ds(start, capacity), :] = picked[...].astype(jnp.bfloat16)

    for position, dz in enumerate(plane_order(dp)):

        @pl.loop(0, rows)
        def _(dr):
            gather(dz * rows + dr)

        if position == 0:
            gathered(dp, rows)

        @pl.loop(0 if dz else 1, rows)
        def _(dr):
            copy(dz, dr, -1).start()

    incoming[0:capacity, :] = outgoing[0:capacity, :]

    lookups = total.shape[0]
    place = jnp.broadcast_to(place_ref[...], (lookups, depth)) - lax.broadcasted_iota(
        jnp.int32, (lookups, depth), 1
    )

    per_plane = rows // group
    for dz in plane_order(dp):

        @pl.loop(0, per_plane)
        def _(step):
            for k in range(group):
                dr = step * group + k

                def arrive():
                    copy(dz, dr, 1).wait_recv()

                if dz == 0:
                    pl.when(dr > 0)(arrive)
                else:
                    arrive()
            start = pl.multiple_of((dz * per_plane + step) * depth, depth)
            chosen = jnp.where(place == start, 1.0, 0.0).astype(jnp.bfloat16)
            total[...] += jnp.dot(
                chosen, incoming[pl.ds(start, depth), :], preferred_element_type=jnp.float32
            )

    next_ref[...] = total[...].astype(jnp.bfloat16)

    for dz in plane_order(dp):

        @pl.loop(0 if dz else 1, rows)
        def _(dr):
            copy(dz, dr, -1).wait_send()


def fetch(dp, rows, wanted, place, table):
    slots = wanted.shape[0]
    devices = dp * rows
    lookups = place.shape[0]
    columns = table.shape[1]
    vmem = pl.BlockSpec(memory_space=pltpu.VMEM)
    hbm = pl.BlockSpec(memory_space=pltpu.HBM)
    return pl.pallas_call(
        functools.partial(fetch_kernel, dp, rows),
        name="fetch",
        out_shape=jax.ShapeDtypeStruct((lookups, columns), jnp.bfloat16),
        in_specs=[hbm, vmem, vmem],
        out_specs=vmem,
        scratch_shapes=[
            pltpu.SMEM((slots,), jnp.int32),
            pltpu.VMEM((slots // devices, columns), jnp.float32),
            pltpu.VMEM((slots, columns), jnp.bfloat16),
            pltpu.VMEM((slots, columns), jnp.bfloat16),
            pltpu.VMEM((lookups, columns), jnp.float32),
            pltpu.SemaphoreType.DMA,
            pltpu.SemaphoreType.DMA((devices,)),
            pltpu.SemaphoreType.DMA((devices,)),
        ],
        compiler_params=pltpu.CompilerParams(
            collective_id=1, has_side_effects=True, vmem_limit_bytes=32 * 1024 * 1024
        ),
    )(wanted, place.reshape(-1, 1), table)


def on_device(owners, offsets, gradients, embedding, adagrad_state, next_owners, next_offsets):
    dp, rows = lax.axis_size("dp"), lax.axis_size("rows")
    devices = dp * rows
    lookups = gradients.shape[0]
    owned = embedding.shape[0]
    capacity = max(2, 4 * lookups // devices)
    z, r = lax.axis_index("dp"), lax.axis_index("rows")

    def relative(names):
        dz = (names // rows - z + dp) % dp
        dr = (names % rows - r + rows) % rows
        return dz * rows + dr

    owner_ids, next_ids = relative(owners[:, 0]), relative(next_owners[:, 0])
    slot_ids, next_slots = positions_of(owner_ids, next_ids, devices)
    places = owner_ids * capacity + slot_ids
    next_places = next_ids * capacity + next_slots
    half = owned // 2
    high = (offsets % half) // SUB
    both = (offsets // half) * SUB + offsets % SUB
    table = slot_table(owner_ids, slot_ids, (high, both), devices, capacity)
    next_table = slot_table(
        next_ids, next_slots, (next_offsets // BASE, next_offsets % BASE), devices, capacity
    )
    meta = jnp.concatenate([table, next_table], axis=1).astype(jnp.bfloat16)
    acc, met = send_gradients(dp, rows, places, gradients, meta, owned)
    wanted = (met[:, 2].astype(jnp.int32) * BASE + met[:, 3].astype(jnp.int32)).reshape(-1)
    new_embedding, new_state, new_table = update(acc, embedding, adagrad_state)
    next_rows = fetch(dp, rows, wanted, next_places, new_table)
    return (new_embedding, new_state, next_rows)


def solution(mesh):
    in_specs = (
        P(("dp", "rows"), None),
        P(("dp", "rows")),
        P(("dp", "rows"), None),
        P(("dp", "rows"), None),
        P(("dp", "rows")),
        P(("dp", "rows"), None),
        P(("dp", "rows")),
    )
    out_specs = (P(("dp", "rows"), None), P(("dp", "rows")), P(("dp", "rows"), None))
    return jax.shard_map(
        on_device, mesh=mesh, in_specs=in_specs, out_specs=out_specs, check_vma=False
    )
```

time: 94.8 us -> 98.3 us (1.037)
  the two profiles are of different devices: /device:TPU:0 before, /device:TPU:9 now
where the time goes in v1:
time: 98.3 us; the launch traced here: 97.9 us
  Pallas kernels  84.4 us (86%)
  other arithmetic  6.1 us (6%)
  local copies, waits for them, and re-layouts  5.54 us (6%)
    pallas_call x1, Pallas kernels, send_gradients(): pl.pallas_call(functools.partial(send_kernel, dp, rows), name='send_gradi...  40.8 us
    pallas_call x1, Pallas kernels, fetch(): pl.pallas_call(functools.partial(fetch_kernel, dp, rows), name='fetch', o...  36.6 us
    pallas_call x1, Pallas kernels, update(): pl.pallas_call(update_kernel, name='update', out_shape=(jax.ShapeDtypeStr...  7.07 us
    unnamed x11, local copies, waits for them, and re-layouts  4.72 us
    add x1, other arithmetic, relative(): return dz * rows + dr  2.04 us

profile of v1, /device:TPU:9, one launch (start us, length us, event | category | flops | bytes accessed | tf_op | source)
XLA Modules:
  0.0 97.9 jit_solution(8970630311280709886)
XLA Ops:
  0.6 0.0 copy-start.3
  0.6 0.7 broadcast_compare_fusion
  1.3 0.7 broadcast_compare_fusion.1
  2.0 0.7 fusion.29
  2.7 0.7 fusion.33
  3.4 0.3 copy.29
  3.7 0.3 copy.36
  4.0 0.9 copy.31
  4.9 0.9 copy.24
  5.9 0.0 copy-start.1
  5.9 2.0 %fusion.49 = (s32[1024]{0:T(1024)S(1)}, s32[1024,1]{1,0:T(8,128)S(1)}, s32[1024]{0:T(1024)S(1)}) fusion(s32[]{:T(128)S(6)} %axis_index.25, s32[]{:T(128)S(6)} %axis_index.23, pred[1024,1]{1,0:T(8,128)(4,1)S(1)} %copy.36, s32[1024,1]{1,0:T(8,128)S(1)} %copy.31, pred[1024,1]{1,0:T(8,128)(4,1)S(1)} %copy.29, s32[1024,1]{1,0:T(8,128)S(1)} %copy.24), kind=kLoop, calls=%fused_computation.124 | loop fusion | flops 94208 | bytes 22536 | tf_op jit(solution)/shard_map/add | solution.py:411
  7.9 0.0 copy-start.2
  8.0 0.6 fusion.1
  8.6 0.0 copy-done.3
  8.6 0.1 multiply_add_fusion.1.place_ref
  8.7 0.5 select_convert_fusion.3
  9.2 0.2 convolution_convert_fusion.1
  9.4 0.5 select_convert_fusion.1
  9.9 0.2 convolution_convert_fusion
  10.2 0.2 copy.38
  10.4 0.1 multiply_add_fusion.place_ref
  10.4 0.0 copy-done.1
  10.5 40.8 %send_gradients.1 = (f32[4096,256]{1,0:T(8,128)S(1)}, bf16[32,4,128]{2,1,0:T(4,128)(2,1)S(1)}) custom-call(s32[1,1024]{1,0:T(1,128)S(1)} %multiply_add_fusion.1.place_ref, bf16[1024,128]{1,0:T(8,128)(2,1)S(1)} %copy-done.1, bf16[32,4,128]{2,1,0:T(4,128)(2,1)S(1)} %pad_maximum_fusion.meta_ref), custom_call_target="tpu_custom_call" | custom-call | tf_op jit(solution)/shard_map/send_gradients/pallas_call | solution.py:204
  51.2 0.1 convert_add_fusion
  51.3 0.0 copy-done.2
  51.3 0.0 copy-start
  51.3 2.2 %copy-done = f32[8192,128]{1,0:T(8,128)S(1)} copy-done((f32[8192,128]{1,0:T(8,128)S(1)}, f32[8192,128]{1,0:T(8,128)}, u32[]{:S(2)}) %copy-start) | copy-done | bytes 4194328
  53.5 7.1 %update.1 = (f32[8192,128]{1,0:T(8,128)}, f32[64,128]{1,0:T(8,128)}, f32[8192,128]{1,0:T(8,128)S(1)}) custom-call(f32[4096,256]{1,0:T(8,128)S(1)} %get-tuple-element.8.acc_ref, f32[8192,128]{1,0:T(8,128)S(1)} %copy-done, f32[64,128]{1,0:T(8,128)S(1)} %bitcast.19), custom_call_target="tpu_custom_call" | custom-call | tf_op jit(solution)/shard_map/update/pallas_call | solution.py:270
  60.6 36.6 %fetch.1 = bf16[1024,128]{1,0:T(8,128)(2,1)S(1)} custom-call(s32[4096]{0:T(1024)S(1)} %bitcast.18, s32[1024,1]{1,0:T(8,128)S(1)} %multiply_add_fusion.place_ref, f32[8192,128]{1,0:T(8,128)S(1)} %get-tuple-element.12.table_ref), custom_call_target="tpu_custom_call" | custom-call | tf_op jit(solution)/shard_map/fetch/pallas_call | solution.py:378
  97.2 0.7 copy.46
  (8 shorter events, 0.2 us)
Async XLA Ops:
  0.6 8.0 %copy-start.3 = (s32[1024,1]{0,1:T(1,128)S(1)}, s32[1024,1]{0,1:T(1,128)}, u32[]{:S(2)}) copy-start(s32[1024,1]{0,1:T(1,128)} %param.7) | copy-start | bytes 12292
  5.9 4.6 %copy-start.1 = (bf16[1024,128]{1,0:T(8,128)(2,1)S(1)}, bf16[1024,128]{1,0:T(8,128)(2,1)}, u32[]{:S(2)}) copy-start(bf16[1024,128]{1,0:T(8,128)(2,1)} %gradients_ref.1) | copy-start | bytes 786436
  7.9 43.4 %copy-start.2 = (f32[8192]{0:T(1024)S(1)}, f32[8192]{0:T(1024)}, u32[]{:S(2)}) copy-start(f32[8192]{0:T(1024)} %param.11) | copy-start | bytes 98308
  51.3 2.2 %copy-start = (f32[8192,128]{1,0:T(8,128)S(1)}, f32[8192,128]{1,0:T(8,128)}, u32[]{:S(2)}) copy-start(f32[8192,128]{1,0:T(8,128)} %embedding_ref.1) | copy-start | bytes 12582916

commit v2 on v1

v2 whole, which is shorter than its diff:
```python
import functools

import jax
import jax.numpy as jnp
from jax import lax
from jax.experimental import pallas as pl
from jax.experimental.pallas import tpu as pltpu
from jax.sharding import PartitionSpec as P

LANES = 128
SUB = 16
BASE = 256
MESH = pl.DeviceIdType.MESH


def flip(value, step, size):
    bit, result = 1, value
    while bit < size:
        own = lax.rem(lax.div(value, bit), 2)
        if isinstance(step, int):
            if step // bit % 2:
                result = result + bit * (1 - 2 * own)
        else:
            other = lax.rem(lax.div(step, bit), 2)
            result = result + bit * other * (1 - 2 * own)
        bit *= 2
    return result


def plane_order(dp):
    return [0, 1] + list(range(dp - 1, 1, -1))


def peer(dp, rows, dz, dr):
    z, r = lax.axis_index("dp"), lax.axis_index("rows")
    return (flip(z, dz, dp), flip(r, dr, rows))


def greet(dp, rows):
    barrier = pltpu.get_barrier_semaphore()
    for i in range(1, dp * rows):
        pl.semaphore_signal(
            barrier, inc=1, device_id=peer(dp, rows, i // rows, i % rows), device_id_type=MESH
        )


def gathered(dp, rows):
    pl.semaphore_wait(pltpu.get_barrier_semaphore(), dp * rows - 1)


def selectors(names, count):
    shape = (SUB, names.shape[1])
    low = lax.broadcasted_iota(jnp.int32, shape, 0) == names % SUB
    ones = jnp.where(low, 1.0, 0.0).astype(jnp.bfloat16)
    high = jnp.broadcast_to((names // SUB).astype(jnp.float32), shape)

    def pick(start):
        shifted = (high - start).astype(jnp.bfloat16)
        zero = jnp.zeros(shape, jnp.bfloat16)
        return jnp.concatenate(
            [jnp.where(shifted == jnp.bfloat16(k), ones, zero) for k in range(count // SUB)], axis=0
        )

    return pick


def route(names, values, me, devices, capacity):
    blocks = names.shape[0]
    columns = names.shape[1]
    relative = jnp.bitwise_xor(names, me)
    index = lax.broadcasted_iota(jnp.int32, (devices, columns), 0)
    hits = [jnp.where(index == relative[b : b + 1, :], 1.0, 0.0) for b in range(blocks)]
    before = jnp.where(
        lax.broadcasted_iota(jnp.int32, (columns, columns), 0)
        < lax.broadcasted_iota(jnp.int32, (columns, columns), 1),
        1.0,
        0.0,
    ).astype(jnp.bfloat16)
    one_hot = [hit.astype(jnp.bfloat16) for hit in hits]
    ahead = jnp.dot(
        jnp.concatenate(one_hot, axis=0), before, preferred_element_type=jnp.float32
    )
    seen = jnp.zeros((devices, 1), jnp.float32)
    slots = []
    for b in range(blocks):
        within = ahead[b * devices : (b + 1) * devices, :] + seen
        slots.append(jnp.sum(hits[b] * within, axis=0, keepdims=True))
        seen = seen + jnp.sum(hits[b], axis=1, keepdims=True)
    slots = jnp.concatenate(slots, axis=0).astype(jnp.int32)
    high = (values // BASE).astype(jnp.float32)
    low = (values % BASE).astype(jnp.float32)
    place = lax.broadcasted_iota(jnp.int32, (capacity, columns), 0)
    marked = []
    for b in range(blocks):
        taken = place == slots[b : b + 1, :]
        marked.append(
            jnp.concatenate(
                [jnp.where(taken, high[b : b + 1, :], 0.0), jnp.where(taken, low[b : b + 1, :], 0.0)],
                axis=0,
            ).astype(jnp.bfloat16)
        )
    table = lax.dot_general(
        jnp.concatenate(one_hot, axis=1),
        jnp.concatenate(marked, axis=1),
        (((1,), (1,)), ((), ())),
        preferred_element_type=jnp.float32,
    )
    table = (table[:, :capacity] * BASE + table[:, capacity:]).astype(jnp.int32)
    return relative * capacity + slots, table


def send_kernel(
    dp, rows,
    owners_ref, offsets_ref, next_owners_ref, next_offsets_ref, gradients_ref,
    acc_ref, met_ref, next_place_ref,
    flat, meta_ref, outgoing, incoming, meta_send, meta_recv, data_send, data_recv,
):
    devices = dp * rows
    slots = outgoing.shape[0]
    capacity = slots // devices
    columns = gradients_ref.shape[1]
    half = acc_ref.shape[0]
    group = 2 if capacity == LANES else 1
    depth = group * capacity

    greet(dp, rows)

    me = lax.axis_index("dp") * rows + lax.axis_index("rows")
    place, table = route(owners_ref[...], offsets_ref[...], me, devices, capacity)
    next_place, next_table = route(
        next_owners_ref[...], next_offsets_ref[...], me, devices, capacity
    )
    next_place_ref[...] = next_place
    flat[...] = jnp.concatenate([table, next_table], axis=1)
    for i in range(devices):
        meta_ref[i] = flat[i : i + 1, :]

    made = min(512, slots)
    pick = selectors(
        jnp.concatenate([place[b : b + 1, :] for b in range(place.shape[0])], axis=1), made
    )

    @pl.loop(0, slots // made)
    def _(step):
        start = pl.multiple_of(step * made, made)
        outgoing[pl.ds(start, made), :] = jnp.dot(
            pick((step * (made // SUB)).astype(jnp.float32)),
            gradients_ref[...],
            preferred_element_type=jnp.float32,
        ).astype(jnp.bfloat16)

    @pl.loop(0, half // LANES)
    def _(step):
        acc_ref[pl.ds(pl.multiple_of(step * LANES, LANES), LANES), :] = jnp.zeros(
            (LANES, acc_ref.shape[1]), jnp.float32
        )

    gathered(dp, rows)

    def copies(dz, dr):
        i = dz * rows + dr
        span = pl.ds(pl.multiple_of(i * capacity, capacity), capacity)
        to = peer(dp, rows, dz, dr)
        meta = pltpu.make_async_remote_copy(
            src_ref=meta_ref.at[i], dst_ref=met_ref.at[i],
            send_sem=meta_send.at[i], recv_sem=meta_recv.at[i],
            device_id=to, device_id_type=MESH,
        )
        data = pltpu.make_async_remote_copy(
            src_ref=outgoing.at[span, :], dst_ref=incoming.at[span, :],
            send_sem=data_send.at[i], recv_sem=data_recv.at[i],
            device_id=to, device_id_type=MESH,
        )
        return meta, data

    for dz in plane_order(dp):
        for dr in range(0 if dz else 1, rows):
            meta, data = copies(dz, dr)
            meta.start()
            data.start()

    met_ref[0] = meta_ref[0]
    incoming[0:capacity, :] = outgoing[0:capacity, :]

    chunk = min(1024, half)

    def accumulate(tile):
        met = [met_ref[tile * group + k][:, :capacity] for k in range(group)]
        parts = []
        for k in range(group):
            side = jnp.broadcast_to((met[k] // half).astype(jnp.float32), (columns, capacity)).T
            start = pl.multiple_of((tile * group + k) * capacity, capacity)
            block = incoming[pl.ds(start, capacity), :].astype(jnp.float32)
            parts.append(
                jnp.concatenate(
                    [jnp.where(side > 0.5, 0.0, block), jnp.where(side > 0.5, block, 0.0)], axis=1
                ).astype(jnp.bfloat16)
            )
        wide = jnp.concatenate(parts, axis=0) if group > 1 else parts[0]
        names = (jnp.concatenate(met, axis=1) if group > 1 else met[0]) % half
        pick_rows = selectors(names, chunk)

        @pl.loop(0, half // chunk)
        def _(step):
            span = pl.ds(pl.multiple_of(step * chunk, chunk), chunk)
            acc_ref[span, :] += jnp.dot(
                pick_rows((step * (chunk // SUB)).astype(jnp.float32)),
                wide,
                preferred_element_type=jnp.float32,
            )

    per_plane = rows // group
    for dz in plane_order(dp):

        @pl.loop(0, per_plane)
        def _(step):
            for k in range(group):
                dr = step * group + k

                def arrive():
                    meta, data = copies(dz, dr)
                    meta.wait_recv()
                    data.wait_recv()

                if dz == 0:
                    pl.when(dr > 0)(arrive)
                else:
                    arrive()
            accumulate(dz * per_plane + step)

    for dz in plane_order(dp):

        @pl.loop(0 if dz else 1, rows)
        def _(dr):
            meta, data = copies(dz, dr)
            meta.wait_send()
            data.wait_send()


def send_gradients(dp, rows, owners, offsets, next_owners, next_offsets, gradients, owned):
    devices = dp * rows
    lookups, columns = gradients.shape
    capacity = max(2, 4 * lookups // devices)
    slots = devices * capacity
    vmem = pl.BlockSpec(memory_space=pltpu.VMEM)
    tiles = (lookups // LANES, LANES)
    return pl.pallas_call(
        functools.partial(send_kernel, dp, rows),
        name="send_gradients",
        out_shape=(
            jax.ShapeDtypeStruct((owned // 2, 2 * columns), jnp.float32),
            jax.ShapeDtypeStruct((devices, 1, 2 * capacity), jnp.int32),
            jax.ShapeDtypeStruct(tiles, jnp.int32),
        ),
        in_specs=[vmem] * 5,
        out_specs=(vmem,) * 3,
        scratch_shapes=[
            pltpu.VMEM((devices, 2 * capacity), jnp.int32),
            pltpu.VMEM((devices, 1, 2 * capacity), jnp.int32),
            pltpu.VMEM((slots, columns), jnp.bfloat16),
            pltpu.VMEM((slots, columns), jnp.bfloat16),
        ]
        + [pltpu.SemaphoreType.DMA((devices,))] * 4,
        compiler_params=pltpu.CompilerParams(
            collective_id=0, has_side_effects=True, vmem_limit_bytes=40 * 1024 * 1024
        ),
        cost_estimate=pl.CostEstimate(
            flops=400 * slots * owned * columns, bytes_accessed=owned * columns * 4, transcendentals=0
        ),
    )(
        owners.reshape(tiles), offsets.reshape(tiles),
        next_owners.reshape(tiles), next_offsets.reshape(tiles),
        gradients,
    )


def update_kernel(
    acc_ref, embedding_ref, state_ref, new_embedding_ref, new_state_ref, table, out_sems
):
    owned = table.shape[0]
    half = acc_ref.shape[0]
    chunks = out_sems.shape[0]
    chunk = owned // chunks

    def store(piece):
        span = pl.ds(piece * chunk, chunk)
        return pltpu.make_async_copy(
            table.at[span, :], new_embedding_ref.at[span, :], out_sems.at[piece]
        )

    for piece in range(chunks):
        side = piece * chunk // half

        @pl.loop(0, chunk // LANES, unroll=4)
        def _(step):
            tile = piece * (chunk // LANES) + step
            span = pl.ds(pl.multiple_of(tile * LANES, LANES), LANES)
            low = pl.ds(pl.multiple_of(tile * LANES - side * half, LANES), LANES)
            grad_sum = acc_ref[low, side * LANES : (side + 1) * LANES]
            mean = jnp.sum(grad_sum * grad_sum, axis=1, keepdims=True) * (1.0 / LANES)
            old = jnp.broadcast_to(state_ref[pl.ds(tile, 1), :], (LANES, LANES)).T
            state = old + mean
            new_state_ref[pl.ds(tile, 1), :] = state.T[0:1, :]
            table[span, :] = embedding_ref[span, :] - 0.5 * grad_sum * lax.rsqrt(state)

        store(piece).start()
    for piece in range(chunks):
        store(piece).wait()


def update(acc, embedding, state):
    owned, columns = embedding.shape
    chunks = 8
    vmem = pl.BlockSpec(memory_space=pltpu.VMEM)
    hbm = pl.BlockSpec(memory_space=pltpu.HBM)
    new_embedding, new_state, table = pl.pallas_call(
        update_kernel,
        name="update",
        out_shape=(
            jax.ShapeDtypeStruct((owned, columns), jnp.float32),
            jax.ShapeDtypeStruct((owned // LANES, LANES), jnp.float32),
            jax.ShapeDtypeStruct((owned, columns), jnp.float32),
        ),
        in_specs=[vmem] * 3,
        out_specs=(hbm, vmem, vmem),
        scratch_shapes=[pltpu.SemaphoreType.DMA((chunks,))],
        compiler_params=pltpu.CompilerParams(vmem_limit_bytes=40 * 1024 * 1024),
    )(acc, embedding, state.reshape(owned // LANES, LANES))
    return new_embedding, new_state.reshape(owned), table


def fetch_kernel(
    dp, rows,
    wanted_hbm, place_ref, table_ref, next_ref,
    wanted_ref, picked, outgoing, incoming, place, total, wanted_sem, data_send, data_recv,
):
    devices = dp * rows
    slots = outgoing.shape[0]
    capacity = slots // devices
    group = 2 if capacity == LANES else 1
    depth = group * capacity

    greet(dp, rows)
    load = pltpu.make_async_copy(wanted_hbm, wanted_ref, wanted_sem)
    load.start()
    total[...] = jnp.zeros(total.shape, jnp.float32)
    for b in range(place_ref.shape[0]):
        row = place_ref[b : b + 1, :].astype(jnp.float32)
        place[b * LANES : (b + 1) * LANES, :] = jnp.broadcast_to(row, (LANES, LANES)).T.astype(
            jnp.int32
        )
    load.wait()

    def copy(dz, dr):
        i = dz * rows + dr
        span = pl.ds(pl.multiple_of(i * capacity, capacity), capacity)
        return pltpu.make_async_remote_copy(
            src_ref=outgoing.at[span, :], dst_ref=incoming.at[span, :],
            send_sem=data_send.at[i], recv_sem=data_recv.at[i],
            device_id=peer(dp, rows, dz, dr), device_id_type=MESH,
        )

    def gather(i):
        start = pl.multiple_of(i * capacity, capacity)
        for k in range(capacity):
            picked[pl.ds(k, 1), :] = table_ref[pl.ds(wanted_ref[start + k], 1), :]
        outgoing[pl.ds(start, capacity), :] = picked[...].astype(jnp.bfloat16)

    for position, dz in enumerate(plane_order(dp)):

        @pl.loop(0, rows)
        def _(dr):
            gather(dz * rows + dr)

        if position == 0:
            gathered(dp, rows)

        for dr in range(0 if dz else 1, rows):
            copy(dz, dr).start()

    incoming[0:capacity, :] = outgoing[0:capacity, :]

    lookups = total.shape[0]

    per_plane = rows // group
    for dz in plane_order(dp):

        @pl.loop(0, per_plane)
        def _(step):
            for k in range(group):
                dr = step * group + k

                def arrive():
                    copy(dz, dr).wait_recv()

                if dz == 0:
                    pl.when(dr > 0)(arrive)
                else:
                    arrive()
            start = pl.multiple_of((dz * per_plane + step) * depth, depth)
            lane = lax.broadcasted_iota(jnp.int32, (lookups, capacity), 1)
            chosen = jnp.concatenate(
                [
                    jnp.where(place[:, :capacity] == lane + (start + k * capacity), 1.0, 0.0)
                    for k in range(group)
                ],
                axis=1,
            ).astype(jnp.bfloat16)
            total[...] += jnp.dot(
                chosen, incoming[pl.ds(start, depth), :], preferred_element_type=jnp.float32
            )

    next_ref[...] = total[...].astype(jnp.bfloat16)

    for dz in plane_order(dp):

        @pl.loop(0 if dz else 1, rows)
        def _(dr):
            copy(dz, dr).wait_send()


def fetch(dp, rows, wanted, place, table):
    slots = wanted.shape[0]
    devices = dp * rows
    lookups = place.shape[0] * place.shape[1]
    columns = table.shape[1]
    vmem = pl.BlockSpec(memory_space=pltpu.VMEM)
    hbm = pl.BlockSpec(memory_space=pltpu.HBM)
    return pl.pallas_call(
        functools.partial(fetch_kernel, dp, rows),
        name="fetch",
        out_shape=jax.ShapeDtypeStruct((lookups, columns), jnp.bfloat16),
        in_specs=[hbm, vmem, vmem],
        out_specs=vmem,
        scratch_shapes=[
            pltpu.SMEM((slots,), jnp.int32),
            pltpu.VMEM((slots // devices, columns), jnp.float32),
            pltpu.VMEM((slots, columns), jnp.bfloat16),
            pltpu.VMEM((slots, columns), jnp.bfloat16),
            pltpu.VMEM((lookups, LANES), jnp.int32),
            pltpu.VMEM((lookups, columns), jnp.float32),
            pltpu.SemaphoreType.DMA,
            pltpu.SemaphoreType.DMA((devices,)),
            pltpu.SemaphoreType.DMA((devices,)),
        ],
        compiler_params=pltpu.CompilerParams(
            collective_id=1, has_side_effects=True, vmem_limit_bytes=32 * 1024 * 1024
        ),
    )(wanted, place, table)


def on_device(owners, offsets, gradients, embedding, adagrad_state, next_owners, next_offsets):
    dp, rows = lax.axis_size("dp"), lax.axis_size("rows")
    acc, met, next_place = send_gradients(
        dp, rows, owners, offsets, next_owners, next_offsets, gradients, embedding.shape[0]
    )
    wanted = met[:, 0, met.shape[2] // 2 :].reshape(-1)
    new_embedding, new_state, new_table = update(acc, embedding, adagrad_state)
    next_rows = fetch(dp, rows, wanted, next_place, new_table)
    return (new_embedding, new_state, next_rows)


def solution(mesh):
    in_specs = (
        P(("dp", "rows"), None),
        P(("dp", "rows")),
        P(("dp", "rows"), None),
        P(("dp", "rows"), None),
        P(("dp", "rows")),
        P(("dp", "rows"), None),
        P(("dp", "rows")),
    )
    out_specs = (P(("dp", "rows"), None), P(("dp", "rows")), P(("dp", "rows"), None))
    return jax.shard_map(
        on_device, mesh=mesh, in_specs=in_specs, out_specs=out_specs, check_vma=False
    )
```

time: 98.3 us -> 83.1 us (0.85)
  the two profiles are of different devices: /device:TPU:9 before, /device:TPU:0 now
where the time goes in v2:
time: 83.1 us; the launch traced here: 82.8 us
  Pallas kernels  77.7 us (94%)
  local copies, waits for them, and re-layouts  4.41 us (5%)
    pallas_call x1, Pallas kernels, send_gradients(): pl.pallas_call(functools.partial(send_kernel, dp, rows), name='send_gradi...  37 us
    pallas_call x1, Pallas kernels, fetch(): pl.pallas_call(functools.partial(fetch_kernel, dp, rows), name='fetch', o...  34 us
    pallas_call x1, Pallas kernels, update(): pl.pallas_call(update_kernel, name='update', out_shape=(jax.ShapeDtypeStr...  6.71 us
    unnamed x15, local copies, waits for them, and re-layouts  4.4 us

profile of v2, /device:TPU:0, one launch (start us, length us, event | category | flops | bytes accessed | tf_op | source)
XLA Modules:
  0.0 82.8 jit_solution(4898213450820679630)
XLA Ops:
  0.6 0.0 copy-start.2
  0.6 0.9 %copy-done.2 = bf16[1024,128]{1,0:T(8,128)(2,1)S(1)} copy-done((bf16[1024,128]{1,0:T(8,128)(2,1)S(1)}, bf16[1024,128]{1,0:T(8,128)(2,1)}, u32[]{:S(2)}) %copy-start.2) | copy-done | bytes 262168
  1.6 0.0 copy-start.3
  1.6 0.7 copy-done.3
  2.3 0.0 copy-start.4
  2.3 0.7 copy-done.4
  3.0 0.0 copy-start.5
  3.0 0.7 copy-done.5
  3.6 0.0 copy-start.6
  3.6 0.7 copy-done.6
  4.3 0.0 copy-start
  4.3 0.0 copy-start.1
  4.3 37.0 %send_gradients.1 = (f32[4096,256]{1,0:T(8,128)S(1)}, s32[32,1,256]{2,1,0:T(1,128)S(1)}, s32[8,128]{1,0:T(8,128)S(1)}) custom-call(s32[8,128]{1,0:T(8,128)S(1)} %bitcast.9, s32[8,128]{1,0:T(8,128)S(1)} %bitcast.10, s32[8,128]{1,0:T(8,128)S(1)} %bitcast.11, s32[8,128]{1,0:T(8,128)S(1)} %bitcast.12, bf16[1024,128]{1,0:T(8,128)(2,1)S(1)} %copy-done.2), custom_call_target="tpu_custom_call" | custom-call | flops 1717986918400 | bytes 4194304 | tf_op jit(solution)/shard_map/send_gradients/pallas_call | solution.py:247
  41.4 0.0 copy-done
  41.4 0.0 copy-done.1
  41.4 6.7 %update.1 = (f32[8192,128]{1,0:T(8,128)}, f32[64,128]{1,0:T(8,128)}, f32[8192,128]{1,0:T(8,128)S(1)}) custom-call(f32[4096,256]{1,0:T(8,128)S(1)} %get-tuple-element.9.acc_ref, f32[8192,128]{1,0:T(8,128)S(1)} %copy-done, f32[64,128]{1,0:T(8,128)S(1)} %bitcast.8), custom_call_target="tpu_custom_call" | custom-call | tf_op jit(solution)/shard_map/update/pallas_call | solution.py:316
  48.1 34.0 %fetch.1 = bf16[1024,128]{1,0:T(8,128)(2,1)S(1)} custom-call(s32[4096]{0:T(1024)S(1)} %bitcast.7, s32[8,128]{1,0:T(8,128)S(1)} %get-tuple-element.13.place_ref, f32[8192,128]{1,0:T(8,128)S(1)} %get-tuple-element.14.table_ref), custom_call_target="tpu_custom_call" | custom-call | tf_op jit(solution)/shard_map/fetch/pallas_call | solution.py:429
  82.1 0.7 copy.11
  (1 shorter events, 0.0 us)
Async XLA Ops:
  0.6 1.0 %copy-start.2 = (bf16[1024,128]{1,0:T(8,128)(2,1)S(1)}, bf16[1024,128]{1,0:T(8,128)(2,1)}, u32[]{:S(2)}) copy-start(bf16[1024,128]{1,0:T(8,128)(2,1)} %gradients_ref.1) | copy-start | bytes 786436
  1.6 0.7 copy-start.3
  2.3 0.7 copy-start.4
  3.0 0.7 copy-start.5
  3.6 0.7 copy-start.6
  4.3 37.1 %copy-start = (f32[8192,128]{1,0:T(8,128)S(1)}, f32[8192,128]{1,0:T(8,128)}, u32[]{:S(2)}) copy-start(f32[8192,128]{1,0:T(8,128)} %embedding_ref.1) | copy-start | bytes 12582916
  4.3 37.1 %copy-start.1 = (f32[8192]{0:T(1024)S(1)}, f32[8192]{0:T(1024)}, u32[]{:S(2)}) copy-start(f32[8192]{0:T(1024)} %param.11) | copy-start | bytes 98308

commit v3 on v2

--- a/solution.py
+++ b/solution.py
@@ -28,7 +28,7 @@
 
 
 def plane_order(dp):
-    return [0, 1] + list(range(dp - 1, 1, -1))
+    return [dp - 1] + list(range(dp - 1))
 
 
 def peer(dp, rows, dz, dr):
@@ -111,7 +111,7 @@
 
 def send_kernel(
     dp, rows,
-    owners_ref, offsets_ref, next_owners_ref, next_offsets_ref, gradients_ref,
+    index_ref, gradients_ref,
     acc_ref, met_ref, next_place_ref,
     flat, meta_ref, outgoing, incoming, meta_send, meta_recv, data_send, data_recv,
 ):
@@ -126,36 +126,17 @@
     greet(dp, rows)
 
     me = lax.axis_index("dp") * rows + lax.axis_index("rows")
-    place, table = route(owners_ref[...], offsets_ref[...], me, devices, capacity)
-    next_place, next_table = route(
-        next_owners_ref[...], next_offsets_ref[...], me, devices, capacity
-    )
+    place, table = route(index_ref[0], index_ref[1], me, devices, capacity)
+    next_place, next_table = route(index_ref[2], index_ref[3], me, devices, capacity)
     next_place_ref[...] = next_place
     flat[...] = jnp.concatenate([table, next_table], axis=1)
     for i in range(devices):
         meta_ref[i] = flat[i : i + 1, :]
 
-    made = min(512, slots)
+    made = min(512, rows * capacity)
     pick = selectors(
         jnp.concatenate([place[b : b + 1, :] for b in range(place.shape[0])], axis=1), made
     )
-
-    @pl.loop(0, slots // made)
-    def _(step):
-        start = pl.multiple_of(step * made, made)
-        outgoing[pl.ds(start, made), :] = jnp.dot(
-            pick((step * (made // SUB)).astype(jnp.float32)),
-            gradients_ref[...],
-            preferred_element_type=jnp.float32,
-        ).astype(jnp.bfloat16)
-
-    @pl.loop(0, half // LANES)
-    def _(step):
-        acc_ref[pl.ds(pl.multiple_of(step * LANES, LANES), LANES), :] = jnp.zeros(
-            (LANES, acc_ref.shape[1]), jnp.float32
-        )
-
-    gathered(dp, rows)
 
     def copies(dz, dr):
         i = dz * rows + dr
@@ -173,11 +154,31 @@
         )
         return meta, data
 
-    for dz in plane_order(dp):
+    plane = rows * capacity
+    for position, dz in enumerate(plane_order(dp)):
+
+        @pl.loop(dz * plane // made, (dz + 1) * plane // made)
+        def _(step):
+            start = pl.multiple_of(step * made, made)
+            outgoing[pl.ds(start, made), :] = jnp.dot(
+                pick((step * (made // SUB)).astype(jnp.float32)),
+                gradients_ref[...],
+                preferred_element_type=jnp.float32,
+            ).astype(jnp.bfloat16)
+
+        if position == 0:
+            gathered(dp, rows)
+
         for dr in range(0 if dz else 1, rows):
             meta, data = copies(dz, dr)
             meta.start()
             data.start()
+
+    @pl.loop(0, half // LANES)
+    def _(step):
+        acc_ref[pl.ds(pl.multiple_of(step * LANES, LANES), LANES), :] = jnp.zeros(
+            (LANES, acc_ref.shape[1]), jnp.float32
+        )
 
     met_ref[0] = meta_ref[0]
     incoming[0:capacity, :] = outgoing[0:capacity, :]
@@ -252,7 +253,7 @@
             jax.ShapeDtypeStruct((devices, 1, 2 * capacity), jnp.int32),
             jax.ShapeDtypeStruct(tiles, jnp.int32),
         ),
-        in_specs=[vmem] * 5,
+        in_specs=[vmem] * 2,
         out_specs=(vmem,) * 3,
         scratch_shapes=[
             pltpu.VMEM((devices, 2 * capacity), jnp.int32),
@@ -268,70 +269,47 @@
             flops=400 * slots * owned * columns, bytes_accessed=owned * columns * 4, transcendentals=0
         ),
     )(
-        owners.reshape(tiles), offsets.reshape(tiles),
-        next_owners.reshape(tiles), next_offsets.reshape(tiles),
+        jnp.stack([part.reshape(tiles) for part in (owners, offsets, next_owners, next_offsets)]),
         gradients,
     )
 
 
-def update_kernel(
-    acc_ref, embedding_ref, state_ref, new_embedding_ref, new_state_ref, table, out_sems
-):
-    owned = table.shape[0]
+def update(acc_ref, embedding_ref, state_ref, new_state_ref, table):
     half = acc_ref.shape[0]
-    chunks = out_sems.shape[0]
-    chunk = owned // chunks
-
-    def store(piece):
-        span = pl.ds(piece * chunk, chunk)
-        return pltpu.make_async_copy(
-            table.at[span, :], new_embedding_ref.at[span, :], out_sems.at[piece]
-        )
-
-    for piece in range(chunks):
-        side = piece * chunk // half
-
-        @pl.loop(0, chunk // LANES, unroll=4)
+    eye = lax.broadcasted_iota(jnp.int32, (LANES, LANES), 0) == lax.broadcasted_iota(
+        jnp.int32, (LANES, LANES), 1
+    )
+    ones = jnp.ones((2 * LANES, LANES), jnp.bfloat16)
+    ones_row = jnp.ones((SUB, 2 * LANES), jnp.bfloat16)
+
+    def split(x):
+        high = x.astype(jnp.bfloat16)
+        return high, (x - high.astype(jnp.float32)).astype(jnp.bfloat16)
+
+    for side in range(table.shape[0] // half):
+
+        @pl.loop(0, half // LANES, unroll=4)
         def _(step):
-            tile = piece * (chunk // LANES) + step
+            tile = side * (half // LANES) + step
             span = pl.ds(pl.multiple_of(tile * LANES, LANES), LANES)
-            low = pl.ds(pl.multiple_of(tile * LANES - side * half, LANES), LANES)
+            low = pl.ds(pl.multiple_of(step * LANES, LANES), LANES)
             grad_sum = acc_ref[low, side * LANES : (side + 1) * LANES]
-            mean = jnp.sum(grad_sum * grad_sum, axis=1, keepdims=True) * (1.0 / LANES)
-            old = jnp.broadcast_to(state_ref[pl.ds(tile, 1), :], (LANES, LANES)).T
-            state = old + mean
-            new_state_ref[pl.ds(tile, 1), :] = state.T[0:1, :]
-            table[span, :] = embedding_ref[span, :] - 0.5 * grad_sum * lax.rsqrt(state)
-
-        store(piece).start()
-    for piece in range(chunks):
-        store(piece).wait()
-
-
-def update(acc, embedding, state):
-    owned, columns = embedding.shape
-    chunks = 8
-    vmem = pl.BlockSpec(memory_space=pltpu.VMEM)
-    hbm = pl.BlockSpec(memory_space=pltpu.HBM)
-    new_embedding, new_state, table = pl.pallas_call(
-        update_kernel,
-        name="update",
-        out_shape=(
-            jax.ShapeDtypeStruct((owned, columns), jnp.float32),
-            jax.ShapeDtypeStruct((owned // LANES, LANES), jnp.float32),
-            jax.ShapeDtypeStruct((owned, columns), jnp.float32),
-        ),
-        in_specs=[vmem] * 3,
-        out_specs=(hbm, vmem, vmem),
-        scratch_shapes=[pltpu.SemaphoreType.DMA((chunks,))],
-        compiler_params=pltpu.CompilerParams(vmem_limit_bytes=40 * 1024 * 1024),
-    )(acc, embedding, state.reshape(owned // LANES, LANES))
-    return new_embedding, new_state.reshape(owned), table
+            square = jnp.concatenate(split(grad_sum * grad_sum), axis=1)
+            mean = lax.dot_general(
+                ones_row, square, (((1,), (1,)), ((), ())), preferred_element_type=jnp.float32
+            )[0:1, :] * (1.0 / LANES)
+            state = state_ref[pl.ds(tile, 1), :] + mean
+            new_state_ref[pl.ds(tile, 1), :] = state
+            scale = jnp.broadcast_to(0.5 * lax.rsqrt(state), (LANES, LANES))
+            diagonal = jnp.concatenate(split(jnp.where(eye, scale, 0.0)), axis=1)
+            rate = jnp.dot(diagonal, ones, preferred_element_type=jnp.float32)
+            table[span, :] = embedding_ref[span, :] - grad_sum * rate
 
 
 def fetch_kernel(
     dp, rows,
-    wanted_hbm, place_ref, table_ref, next_ref,
+    wanted_hbm, place_ref, acc_ref, embedding_ref, state_ref,
+    table, new_state_ref, next_ref,
     wanted_ref, picked, outgoing, incoming, place, total, wanted_sem, data_send, data_recv,
 ):
     devices = dp * rows
@@ -343,12 +321,7 @@
     greet(dp, rows)
     load = pltpu.make_async_copy(wanted_hbm, wanted_ref, wanted_sem)
     load.start()
-    total[...] = jnp.zeros(total.shape, jnp.float32)
-    for b in range(place_ref.shape[0]):
-        row = place_ref[b : b + 1, :].astype(jnp.float32)
-        place[b * LANES : (b + 1) * LANES, :] = jnp.broadcast_to(row, (LANES, LANES)).T.astype(
-            jnp.int32
-        )
+    update(acc_ref, embedding_ref, state_ref, new_state_ref, table)
     load.wait()
 
     def copy(dz, dr):
@@ -363,25 +336,33 @@
     def gather(i):
         start = pl.multiple_of(i * capacity, capacity)
         for k in range(capacity):
-            picked[pl.ds(k, 1), :] = table_ref[pl.ds(wanted_ref[start + k], 1), :]
+            picked[pl.ds(k, 1), :] = table[pl.ds(wanted_ref[start + k], 1), :]
         outgoing[pl.ds(start, capacity), :] = picked[...].astype(jnp.bfloat16)
 
     for position, dz in enumerate(plane_order(dp)):
-
-        @pl.loop(0, rows)
+        gather(dz * rows)
+        if position == 0:
+            gathered(dp, rows)
+
+        @pl.loop(1, rows)
         def _(dr):
             gather(dz * rows + dr)
-
-        if position == 0:
-            gathered(dp, rows)
-
-        for dr in range(0 if dz else 1, rows):
-            copy(dz, dr).start()
+            if dz:
+                copy(dz, dr - 1).start()
+            else:
+                pl.when(dr > 1)(lambda: copy(dz, dr - 1).start())
+
+        copy(dz, rows - 1).start()
 
     incoming[0:capacity, :] = outgoing[0:capacity, :]
+    total[...] = jnp.zeros(total.shape, jnp.float32)
+    for b in range(place_ref.shape[0]):
+        row = place_ref[b : b + 1, :].astype(jnp.float32)
+        place[b * LANES : (b + 1) * LANES, :] = jnp.broadcast_to(row, (LANES, LANES)).T.astype(
+            jnp.int32
+        )
 
     lookups = total.shape[0]
-
     per_plane = rows // group
     for dz in plane_order(dp):
 
@@ -419,19 +400,24 @@
             copy(dz, dr).wait_send()
 
 
-def fetch(dp, rows, wanted, place, table):
+def fetch(dp, rows, wanted, place, acc, embedding, state):
     slots = wanted.shape[0]
     devices = dp * rows
     lookups = place.shape[0] * place.shape[1]
-    columns = table.shape[1]
+    owned, columns = embedding.shape
+    tiles = (owned // LANES, LANES)
     vmem = pl.BlockSpec(memory_space=pltpu.VMEM)
     hbm = pl.BlockSpec(memory_space=pltpu.HBM)
-    return pl.pallas_call(
+    table, new_state, next_rows = pl.pallas_call(
         functools.partial(fetch_kernel, dp, rows),
         name="fetch",
-        out_shape=jax.ShapeDtypeStruct((lookups, columns), jnp.bfloat16),
-        in_specs=[hbm, vmem, vmem],
-        out_specs=vmem,
+        out_shape=(
+            jax.ShapeDtypeStruct((owned, columns), jnp.float32),
+            jax.ShapeDtypeStruct(tiles, jnp.float32),
+            jax.ShapeDtypeStruct((lookups, columns), jnp.bfloat16),
+        ),
+        in_specs=[hbm] + [vmem] * 4,
+        out_specs=(vmem,) * 3,
         scratch_shapes=[
             pltpu.SMEM((slots,), jnp.int32),
             pltpu.VMEM((slots // devices, columns), jnp.float32),
@@ -444,9 +430,10 @@
             pltpu.SemaphoreType.DMA((devices,)),
         ],
         compiler_params=pltpu.CompilerParams(
-            collective_id=1, has_side_effects=True, vmem_limit_bytes=32 * 1024 * 1024
+            collective_id=1, has_side_effects=True, vmem_limit_bytes=40 * 1024 * 1024
         ),
-    )(wanted, place, table)
+    )(wanted, place, acc, embedding, state.reshape(tiles))
+    return table, new_state.reshape(owned), next_rows
 
 
 def on_device(owners, offsets, gradients, embedding, adagrad_state, next_owners, next_offsets):
@@ -455,8 +442,9 @@
         dp, rows, owners, offsets, next_owners, next_offsets, gradients, embedding.shape[0]
     )
     wanted = met[:, 0, met.shape[2] // 2 :].reshape(-1)
-    new_embedding, new_state, new_table = update(acc, embedding, adagrad_state)
-    next_rows = fetch(dp, rows, wanted, next_place, new_table)
+    new_embedding, new_state, next_rows = fetch(
+        dp, rows, wanted, next_place, acc, embedding, adagrad_state
+    )
     return (new_embedding, new_state, next_rows)
 
 

time: 83.1 us -> 83.5 us (level)
    pallas_call x1, Pallas kernels: 34 us -> 43.1 us  [fetch(): pl.pallas_call(functools.partial(fetch_kernel, dp, rows), name='fetch', o...]
    pallas_call x1 -> x0, Pallas kernels: 6.71 us -> none  [update(): pl.pallas_call(update_kernel, name='update', out_shape=(jax.ShapeDtypeStr...]
    pallas_call x1, Pallas kernels: 37 us -> 34.6 us  [send_gradients(): pl.pallas_call(functools.partial(send_kernel, dp, rows), name='send_gradi...]
    unnamed x15 -> x9, local copies, waits for them, and re-layouts: 4.4 us -> 4.29 us
where the time goes in v3:
time: 83.5 us; the launch traced here: 83.4 us
  Pallas kernels  77.6 us (93%)
  local copies, waits for them, and re-layouts  4.3 us (5%)
    pallas_call x1, Pallas kernels, fetch(): pl.pallas_call(functools.partial(fetch_kernel, dp, rows), name='fetch', o...  43.1 us
    pallas_call x1, Pallas kernels, send_gradients(): pl.pallas_call(functools.partial(send_kernel, dp, rows), name='send_gradi...  34.6 us
    unnamed x9, local copies, waits for them, and re-layouts  4.29 us

profile of v3, /device:TPU:0, one launch (start us, length us, event | category | flops | bytes accessed | tf_op | source)
XLA Modules:
  0.0 83.4 jit_solution(16780926390431948219)
XLA Ops:
  0.6 0.7 pad_add_fusion.index_ref
  1.4 0.0 copy-start.2
  1.4 0.9 %copy-done.2 = bf16[1024,128]{1,0:T(8,128)(2,1)S(1)} copy-done((bf16[1024,128]{1,0:T(8,128)(2,1)S(1)}, bf16[1024,128]{1,0:T(8,128)(2,1)}, u32[]{:S(2)}) %copy-start.2) | copy-done | bytes 262168
  2.3 0.0 copy-start
  2.3 0.0 copy-start.1
  2.3 34.6 %send_gradients.1 = (f32[4096,256]{1,0:T(8,128)S(1)}, s32[32,1,256]{2,1,0:T(1,128)S(1)}, s32[8,128]{1,0:T(8,128)S(1)}) custom-call(s32[4,8,128]{2,1,0:T(8,128)S(1)} %pad_add_fusion.index_ref, bf16[1024,128]{1,0:T(8,128)(2,1)S(1)} %copy-done.2), custom_call_target="tpu_custom_call" | custom-call | flops 1717986918400 | bytes 4194304 | tf_op jit(solution)/shard_map/send_gradients/pallas_call | solution.py:248
  36.9 0.0 copy-done
  36.9 0.0 copy-done.1
  37.0 43.1 %fetch.1 = (f32[8192,128]{1,0:T(8,128)S(1)}, f32[64,128]{1,0:T(8,128)S(1)}, bf16[1024,128]{1,0:T(8,128)(2,1)S(1)}) custom-call(s32[4096]{0:T(1024)S(1)} %bitcast.7, s32[8,128]{1,0:T(8,128)S(1)} %get-tuple-element.10.place_ref, f32[4096,256]{1,0:T(8,128)S(1)} %get-tuple-element.11.acc_ref, f32[8192,128]{1,0:T(8,128)S(1)} %copy-done, f32[64,128]{1,0:T(8,128)S(1)} %bitcast.8), custom_call_target="tpu_custom_call" | custom-call | tf_op jit(solution)/shard_map/fetch/pallas_call | solution.py:411
  80.0 2.0 %copy.13 = f32[8192,128]{1,0:T(8,128)} copy(f32[8192,128]{1,0:T(8,128)S(1)} %get-tuple-element.18) | data formatting | bytes 8388608
  82.0 0.6 copy.14
  82.6 0.7 copy.15
  (1 shorter events, 0.0 us)
Async XLA Ops:
  1.4 0.9 %copy-start.2 = (bf16[1024,128]{1,0:T(8,128)(2,1)S(1)}, bf16[1024,128]{1,0:T(8,128)(2,1)}, u32[]{:S(2)}) copy-start(bf16[1024,128]{1,0:T(8,128)(2,1)} %gradients_ref.1) | copy-start | bytes 786436
  2.3 34.6 %copy-start = (f32[8192,128]{1,0:T(8,128)S(1)}, f32[8192,128]{1,0:T(8,128)}, u32[]{:S(2)}) copy-start(f32[8192,128]{1,0:T(8,128)} %embedding_ref.1) | copy-start | bytes 12582916
  2.3 34.6 %copy-start.1 = (f32[8192]{0:T(1024)S(1)}, f32[8192]{0:T(1024)}, u32[]{:S(2)}) copy-start(f32[8192]{0:T(1024)} %param.11) | copy-start | bytes 98308

commit v4 on v3

--- a/solution.py
+++ b/solution.py
@@ -274,35 +274,62 @@
     )
 
 
-def update(acc_ref, embedding_ref, state_ref, new_state_ref, table):
+def split(x):
+    high = x.astype(jnp.bfloat16)
+    return high, (x - high.astype(jnp.float32)).astype(jnp.bfloat16)
+
+
+def update(acc_ref, embedding_ref, state_ref, new_state_ref, rate_ref, table):
     half = acc_ref.shape[0]
+    tiles = half // LANES
     eye = lax.broadcasted_iota(jnp.int32, (LANES, LANES), 0) == lax.broadcasted_iota(
         jnp.int32, (LANES, LANES), 1
     )
+    same = jnp.where(eye, 1.0, 0.0).astype(jnp.bfloat16)
     ones = jnp.ones((2 * LANES, LANES), jnp.bfloat16)
-    ones_row = jnp.ones((SUB, 2 * LANES), jnp.bfloat16)
-
-    def split(x):
-        high = x.astype(jnp.bfloat16)
-        return high, (x - high.astype(jnp.float32)).astype(jnp.bfloat16)
-
-    for side in range(table.shape[0] // half):
-
-        @pl.loop(0, half // LANES, unroll=4)
+    sides = table.shape[0] // half
+
+    batch = min(8, tiles)
+
+    for side in range(sides):
+
+        @pl.loop(0, tiles // batch)
         def _(step):
-            tile = side * (half // LANES) + step
-            span = pl.ds(pl.multiple_of(tile * LANES, LANES), LANES)
-            low = pl.ds(pl.multiple_of(step * LANES, LANES), LANES)
+            low = pl.ds(pl.multiple_of(step * batch * LANES, batch * LANES), batch * LANES)
             grad_sum = acc_ref[low, side * LANES : (side + 1) * LANES]
             square = jnp.concatenate(split(grad_sum * grad_sum), axis=1)
-            mean = lax.dot_general(
-                ones_row, square, (((1,), (1,)), ((), ())), preferred_element_type=jnp.float32
-            )[0:1, :] * (1.0 / LANES)
-            state = state_ref[pl.ds(tile, 1), :] + mean
-            new_state_ref[pl.ds(tile, 1), :] = state
-            scale = jnp.broadcast_to(0.5 * lax.rsqrt(state), (LANES, LANES))
-            diagonal = jnp.concatenate(split(jnp.where(eye, scale, 0.0)), axis=1)
+            sums = jnp.dot(square, ones, preferred_element_type=jnp.float32)
+            means = [
+                jnp.sum(
+                    jnp.where(eye, sums[k * LANES : (k + 1) * LANES, :], 0.0), axis=0, keepdims=True
+                )
+                for k in range(batch)
+            ]
+            first = pl.multiple_of(side * tiles + step * batch, batch)
+            rate_ref[pl.ds(first, batch), :] = jnp.concatenate(means, axis=0)
+
+    state = state_ref[...] + rate_ref[...] * (1.0 / LANES)
+    new_state_ref[...] = state
+    rate_ref[...] = 0.5 * lax.rsqrt(state)
+
+    for side in range(sides):
+
+        @pl.loop(0, tiles // batch)
+        def _(step):
+            first = pl.multiple_of(side * tiles + step * batch, batch)
+            rows = batch * LANES
+            span = pl.ds(pl.multiple_of(first * LANES, rows), rows)
+            low = pl.ds(pl.multiple_of(step * rows, rows), rows)
+            parts = split(rate_ref[pl.ds(first, batch), :])
+            diagonal = jnp.concatenate(
+                [
+                    jnp.concatenate([same * part[k : k + 1, :] for part in parts], axis=1)
+                    for k in range(batch)
+                ],
+                axis=0,
+            )
             rate = jnp.dot(diagonal, ones, preferred_element_type=jnp.float32)
+            grad_sum = acc_ref[low, side * LANES : (side + 1) * LANES]
             table[span, :] = embedding_ref[span, :] - grad_sum * rate
 
 
@@ -310,7 +337,7 @@
     dp, rows,
     wanted_hbm, place_ref, acc_ref, embedding_ref, state_ref,
     table, new_state_ref, next_ref,
-    wanted_ref, picked, outgoing, incoming, place, total, wanted_sem, data_send, data_recv,
+    wanted_ref, picked, outgoing, incoming, place, total, rate_ref, wanted_sem, data_send, data_recv,
 ):
     devices = dp * rows
     slots = outgoing.shape[0]
@@ -321,7 +348,7 @@
     greet(dp, rows)
     load = pltpu.make_async_copy(wanted_hbm, wanted_ref, wanted_sem)
     load.start()
-    update(acc_ref, embedding_ref, state_ref, new_state_ref, table)
+    update(acc_ref, embedding_ref, state_ref, new_state_ref, rate_ref, table)
     load.wait()
 
     def copy(dz, dr):
@@ -398,6 +425,39 @@
         @pl.loop(0 if dz else 1, rows)
         def _(dr):
             copy(dz, dr).wait_send()
+
+
+def finish_kernel(*refs):
+    count = len(refs) // 2
+    sems = refs[-1]
+    copies = []
+    for source, target in zip(refs[:count], refs[count:-1]):
+        pieces = 8 if source.shape[0] > 4096 else 1
+        size = source.shape[0] // pieces
+        for piece in range(pieces):
+            span = pl.ds(piece * size, size)
+            copies.append(
+                pltpu.make_async_copy(
+                    source.at[span, :], target.at[span, :], sems.at[len(copies)]
+                )
+            )
+            copies[-1].start()
+    for copy in copies:
+        copy.wait()
+
+
+def finish(*arrays):
+    vmem = pl.BlockSpec(memory_space=pltpu.VMEM)
+    hbm = pl.BlockSpec(memory_space=pltpu.HBM)
+    return pl.pallas_call(
+        finish_kernel,
+        name="finish",
+        out_shape=tuple(jax.ShapeDtypeStruct(array.shape, array.dtype) for array in arrays),
+        in_specs=[vmem] * len(arrays),
+        out_specs=(hbm,) * len(arrays),
+        scratch_shapes=[pltpu.SemaphoreType.DMA((8 + len(arrays),))],
+        compiler_params=pltpu.CompilerParams(vmem_limit_bytes=16 * 1024 * 1024),
+    )(*arrays)
 
 
 def fetch(dp, rows, wanted, place, acc, embedding, state):
@@ -425,6 +485,7 @@
             pltpu.VMEM((slots, columns), jnp.bfloat16),
             pltpu.VMEM((lookups, LANES), jnp.int32),
             pltpu.VMEM((lookups, columns), jnp.float32),
+            pltpu.VMEM(tiles, jnp.float32),
             pltpu.SemaphoreType.DMA,
             pltpu.SemaphoreType.DMA((devices,)),
             pltpu.SemaphoreType.DMA((devices,)),
@@ -433,7 +494,8 @@
             collective_id=1, has_side_effects=True, vmem_limit_bytes=40 * 1024 * 1024
         ),
     )(wanted, place, acc, embedding, state.reshape(tiles))
-    return table, new_state.reshape(owned), next_rows
+    new_embedding, new_state, next_rows = finish(table, new_state, next_rows)
+    return new_embedding, new_state.reshape(owned), next_rows
 
 
 def on_device(owners, offsets, gradients, embedding, adagrad_state, next_owners, next_offsets):

time: 83.5 us -> 76.1 us (0.911)
  Pallas kernels: 77.6 us -> 73.5 us
  local copies, waits for them, and re-layouts: 4.3 us -> 0.97 us
    pallas_call x1, Pallas kernels: 43.1 us -> 36.7 us  [fetch(): pl.pallas_call(functools.partial(fetch_kernel, dp, rows), name='fetch', o...]
    unnamed x9 -> x6, local copies, waits for them, and re-layouts: 4.29 us -> 0.96 us
    pallas_call x0 -> x1, Pallas kernels: none -> 2.19 us  [finish(): pl.pallas_call(finish_kernel, name='finish', out_shape=tuple((jax.ShapeDt...]
where the time goes in v4:
time: 76.1 us; the launch traced here: 75.9 us
  Pallas kernels  73.5 us (97%)
  local copies, waits for them, and re-layouts  0.97 us (1%)
    pallas_call x1, Pallas kernels, fetch(): pl.pallas_call(functools.partial(fetch_kernel, dp, rows), name='fetch', o...  36.7 us
    pallas_call x1, Pallas kernels, send_gradients(): pl.pallas_call(functools.partial(send_kernel, dp, rows), name='send_gradi...  34.6 us
    pallas_call x1, Pallas kernels, finish(): pl.pallas_call(finish_kernel, name='finish', out_shape=tuple((jax.ShapeDt...  2.19 us

profile of v4, /device:TPU:0, one launch (start us, length us, event | category | flops | bytes accessed | tf_op | source)
XLA Modules:
  0.0 75.9 jit_solution(16201545550609938375)
XLA Ops:
  0.6 0.7 pad_add_fusion.index_ref
  1.4 0.0 copy-start.2
  1.4 0.9 %copy-done.2 = bf16[1024,128]{1,0:T(8,128)(2,1)S(1)} copy-done((bf16[1024,128]{1,0:T(8,128)(2,1)S(1)}, bf16[1024,128]{1,0:T(8,128)(2,1)}, u32[]{:S(2)}) %copy-start.2) | copy-done | bytes 262168
  2.3 0.0 copy-start
  2.3 0.0 copy-start.1
  2.3 34.6 %send_gradients.1 = (f32[4096,256]{1,0:T(8,128)S(1)}, s32[32,1,256]{2,1,0:T(1,128)S(1)}, s32[8,128]{1,0:T(8,128)S(1)}) custom-call(s32[4,8,128]{2,1,0:T(8,128)S(1)} %pad_add_fusion.index_ref, bf16[1024,128]{1,0:T(8,128)(2,1)S(1)} %copy-done.2), custom_call_target="tpu_custom_call" | custom-call | flops 1717986918400 | bytes 4194304 | tf_op jit(solution)/shard_map/send_gradients/pallas_call | solution.py:248
  36.9 0.0 copy-done
  36.9 0.0 copy-done.1
  37.0 36.7 %fetch.1 = (f32[8192,128]{1,0:T(8,128)S(1)}, f32[64,128]{1,0:T(8,128)S(1)}, bf16[1024,128]{1,0:T(8,128)(2,1)S(1)}) custom-call(s32[4096]{0:T(1024)S(1)} %bitcast.7, s32[8,128]{1,0:T(8,128)S(1)} %get-tuple-element.13.place_ref, f32[4096,256]{1,0:T(8,128)S(1)} %get-tuple-element.14.acc_ref, f32[8192,128]{1,0:T(8,128)S(1)} %copy-done, f32[64,128]{1,0:T(8,128)S(1)} %bitcast.8), custom_call_target="tpu_custom_call" | custom-call | tf_op jit(solution)/shard_map/fetch/pallas_call | solution.py:471
  73.7 2.2 %finish.1 = (f32[8192,128]{1,0:T(8,128)}, f32[64,128]{1,0:T(8,128)}, bf16[1024,128]{1,0:T(8,128)(2,1)}) custom-call(f32[8192,128]{1,0:T(8,128)S(1)} %get-tuple-element.15.refs_0_, f32[64,128]{1,0:T(8,128)S(1)} %get-tuple-element.16.refs_1_, bf16[1024,128]{1,0:T(8,128)(2,1)S(1)} %get-tuple-element.17.refs_2_), custom_call_target="tpu_custom_call" | custom-call | tf_op jit(solution)/shard_map/finish/pallas_call | solution.py:452
  (1 shorter events, 0.0 us)
Async XLA Ops:
  1.4 0.9 %copy-start.2 = (bf16[1024,128]{1,0:T(8,128)(2,1)S(1)}, bf16[1024,128]{1,0:T(8,128)(2,1)}, u32[]{:S(2)}) copy-start(bf16[1024,128]{1,0:T(8,128)(2,1)} %gradients_ref.1) | copy-start | bytes 786436
  2.3 34.6 %copy-start = (f32[8192,128]{1,0:T(8,128)S(1)}, f32[8192,128]{1,0:T(8,128)}, u32[]{:S(2)}) copy-start(f32[8192,128]{1,0:T(8,128)} %embedding_ref.1) | copy-start | bytes 12582916
  2.3 34.6 %copy-start.1 = (f32[8192]{0:T(1024)S(1)}, f32[8192]{0:T(1024)}, u32[]{:S(2)}) copy-start(f32[8192]{0:T(1024)} %param.11) | copy-start | bytes 98308

commit v5 on v4

--- a/solution.py
+++ b/solution.py
@@ -27,8 +27,8 @@
     return result
 
 
-def plane_order(dp):
-    return [dp - 1] + list(range(dp - 1))
+def is_inner(dp):
+    return lax.rem(lax.div(lax.axis_index("dp") + 1, 2), 2)
 
 
 def peer(dp, rows, dz, dr):
@@ -112,8 +112,9 @@
 def send_kernel(
     dp, rows,
     index_ref, gradients_ref,
-    acc_ref, met_ref, next_place_ref,
-    flat, meta_ref, outgoing, incoming, meta_send, meta_recv, data_send, data_recv,
+    acc_ref, met_ref, places_ref, relayed_ref,
+    flat, meta_ref, outgoing, incoming, raw, relay_out,
+    meta_send, meta_recv, data_send, data_recv, relay_send, raw_sems,
 ):
     devices = dp * rows
     slots = outgoing.shape[0]
@@ -128,51 +129,110 @@
     me = lax.axis_index("dp") * rows + lax.axis_index("rows")
     place, table = route(index_ref[0], index_ref[1], me, devices, capacity)
     next_place, next_table = route(index_ref[2], index_ref[3], me, devices, capacity)
-    next_place_ref[...] = next_place
+    places_ref[0] = place
+    places_ref[1] = next_place
     flat[...] = jnp.concatenate([table, next_table], axis=1)
     for i in range(devices):
         meta_ref[i] = flat[i : i + 1, :]
 
-    made = min(512, rows * capacity)
-    pick = selectors(
-        jnp.concatenate([place[b : b + 1, :] for b in range(place.shape[0])], axis=1), made
-    )
-
-    def copies(dz, dr):
+    inner = is_inner(dp)
+    plane = rows * capacity
+    made = min(512, plane)
+
+    def builder(place):
+        return selectors(
+            jnp.concatenate([place[b : b + 1, :] for b in range(place.shape[0])], axis=1), made
+        )
+
+    def build(pick, source, target, dz, base):
+        @pl.loop(0, plane // made)
+        def _(step):
+            first = dz * plane + step * made
+            target[pl.ds(pl.multiple_of(first - base, made), made), :] = jnp.dot(
+                pick(jnp.float32(first // SUB) if isinstance(first, int)
+                     else (first // SUB).astype(jnp.float32)),
+                source[...],
+                preferred_element_type=jnp.float32,
+            ).astype(jnp.bfloat16)
+
+    def span_of(i):
+        return pl.ds(pl.multiple_of(i * capacity, capacity), capacity)
+
+    def send_meta(dz, dr):
         i = dz * rows + dr
-        span = pl.ds(pl.multiple_of(i * capacity, capacity), capacity)
-        to = peer(dp, rows, dz, dr)
-        meta = pltpu.make_async_remote_copy(
+        return pltpu.make_async_remote_copy(
             src_ref=meta_ref.at[i], dst_ref=met_ref.at[i],
             send_sem=meta_send.at[i], recv_sem=meta_recv.at[i],
-            device_id=to, device_id_type=MESH,
-        )
-        data = pltpu.make_async_remote_copy(
-            src_ref=outgoing.at[span, :], dst_ref=incoming.at[span, :],
+            device_id=peer(dp, rows, dz, dr), device_id_type=MESH,
+        )
+
+    def send_data(dz, dr):
+        i = dz * rows + dr
+        return pltpu.make_async_remote_copy(
+            src_ref=outgoing.at[span_of(i), :], dst_ref=incoming.at[span_of(i), :],
             send_sem=data_send.at[i], recv_sem=data_recv.at[i],
-            device_id=to, device_id_type=MESH,
-        )
-        return meta, data
-
-    plane = rows * capacity
-    for position, dz in enumerate(plane_order(dp)):
-
-        @pl.loop(dz * plane // made, (dz + 1) * plane // made)
-        def _(step):
-            start = pl.multiple_of(step * made, made)
-            outgoing[pl.ds(start, made), :] = jnp.dot(
-                pick((step * (made // SUB)).astype(jnp.float32)),
-                gradients_ref[...],
-                preferred_element_type=jnp.float32,
-            ).astype(jnp.bfloat16)
-
-        if position == 0:
-            gathered(dp, rows)
-
+            device_id=peer(dp, rows, dz, dr), device_id_type=MESH,
+        )
+
+    def relay_data(dz, dr):
+        i = dz * rows + dr
+        k = i - 2 * rows
+        return pltpu.make_async_remote_copy(
+            src_ref=relay_out.at[span_of(k), :], dst_ref=incoming.at[span_of(i), :],
+            send_sem=relay_send.at[k], recv_sem=data_recv.at[i],
+            device_id=peer(dp, rows, dz - 2, dr), device_id_type=MESH,
+        )
+
+    def send_raw():
+        to = peer(dp, rows, 2, 0)
+        return (
+            pltpu.make_async_remote_copy(
+                src_ref=places_ref, dst_ref=relayed_ref,
+                send_sem=raw_sems.at[0], recv_sem=raw_sems.at[1],
+                device_id=to, device_id_type=MESH,
+            ),
+            pltpu.make_async_remote_copy(
+                src_ref=gradients_ref, dst_ref=raw,
+                send_sem=raw_sems.at[2], recv_sem=raw_sems.at[3],
+                device_id=to, device_id_type=MESH,
+            ),
+        )
+
+    pick = builder(place)
+
+    @pl.when(inner == 1)
+    def _():
+        build(pick, gradients_ref, outgoing, 2, 0)
+
+    gathered(dp, rows)
+
+    @pl.when(inner == 0)
+    def _():
+        for copy in send_raw():
+            copy.start()
+
+    for dz in (2, 1, 3, 0):
         for dr in range(0 if dz else 1, rows):
-            meta, data = copies(dz, dr)
-            meta.start()
-            data.start()
+            send_meta(dz, dr).start()
+
+    def send_plane(dz):
+        for dr in range(0 if dz else 1, rows):
+            send_data(dz, dr).start()
+
+    @pl.when(inner == 1)
+    def _():
+        send_plane(2)
+
+    build(pick, gradients_ref, outgoing, 1, 0)
+    send_plane(1)
+
+    @pl.when(inner == 1)
+    def _():
+        build(pick, gradients_ref, outgoing, 3, 0)
+        send_plane(3)
+
+    build(pick, gradients_ref, outgoing, 0, 0)
+    send_plane(0)
 
     @pl.loop(0, half // LANES)
     def _(step):
@@ -211,31 +271,71 @@
             )
 
     per_plane = rows // group
-    for dz in plane_order(dp):
-
+
+    def take_plane(dz):
         @pl.loop(0, per_plane)
         def _(step):
             for k in range(group):
                 dr = step * group + k
 
+                def arrive_meta():
+                    send_meta(dz, dr).wait_recv()
+
                 def arrive():
-                    meta, data = copies(dz, dr)
-                    meta.wait_recv()
-                    data.wait_recv()
+                    send_data(dz, dr).wait_recv()
 
                 if dz == 0:
+                    pl.when(dr > 0)(arrive_meta)
                     pl.when(dr > 0)(arrive)
+                elif dz == 2:
+                    arrive_meta()
+                    pl.when(dr + (1 - inner) > 0)(arrive)
                 else:
+                    arrive_meta()
                     arrive()
             accumulate(dz * per_plane + step)
 
-    for dz in plane_order(dp):
+    take_plane(0)
+    take_plane(1)
+
+    @pl.when(inner == 1)
+    def _():
+        for copy in send_raw():
+            copy.wait_recv()
+        relay_pick = builder(relayed_ref[0])
+        for dz in (3, 2):
+            build(relay_pick, raw, relay_out, dz, 2 * plane)
+            for dr in range(0 if dz == 3 else 1, rows):
+                relay_data(dz, dr).start()
+        incoming[2 * plane : 2 * plane + capacity, :] = relay_out[0:capacity, :]
+
+    take_plane(2)
+    take_plane(3)
+
+    for dz in range(dp):
 
         @pl.loop(0 if dz else 1, rows)
         def _(dr):
-            meta, data = copies(dz, dr)
-            meta.wait_send()
-            data.wait_send()
+            send_meta(dz, dr).wait_send()
+            if dz < 2:
+                send_data(dz, dr).wait_send()
+
+    @pl.when(inner == 1)
+    def _():
+        for dz in (2, 3):
+
+            @pl.loop(0, rows)
+            def _(dr):
+                send_data(dz, dr).wait_send()
+
+            @pl.loop(0 if dz == 3 else 1, rows)
+            def _(dr):
+                relay_data(dz, dr).wait_send()
+
+    @pl.when(inner == 0)
+    def _():
+        for copy in send_raw():
+            copy.wait_send()
 
 
 def send_gradients(dp, rows, owners, offsets, next_owners, next_offsets, gradients, owned):
@@ -251,17 +351,21 @@
         out_shape=(
             jax.ShapeDtypeStruct((owned // 2, 2 * columns), jnp.float32),
             jax.ShapeDtypeStruct((devices, 1, 2 * capacity), jnp.int32),
-            jax.ShapeDtypeStruct(tiles, jnp.int32),
+            jax.ShapeDtypeStruct((2,) + tiles, jnp.int32),
+            jax.ShapeDtypeStruct((2,) + tiles, jnp.int32),
         ),
         in_specs=[vmem] * 2,
-        out_specs=(vmem,) * 3,
+        out_specs=(vmem,) * 4,
         scratch_shapes=[
             pltpu.VMEM((devices, 2 * capacity), jnp.int32),
             pltpu.VMEM((devices, 1, 2 * capacity), jnp.int32),
             pltpu.VMEM((slots, columns), jnp.bfloat16),
             pltpu.VMEM((slots, columns), jnp.bfloat16),
+            pltpu.VMEM((lookups, columns), jnp.bfloat16),
+            pltpu.VMEM((2 * rows * capacity, columns), jnp.bfloat16),
         ]
-        + [pltpu.SemaphoreType.DMA((devices,))] * 4,
+        + [pltpu.SemaphoreType.DMA((devices,))] * 4
+        + [pltpu.SemaphoreType.DMA((2 * rows,)), pltpu.SemaphoreType.DMA((4,))],
         compiler_params=pltpu.CompilerParams(
             collective_id=0, has_side_effects=True, vmem_limit_bytes=40 * 1024 * 1024
         ),
@@ -335,9 +439,10 @@
 
 def fetch_kernel(
     dp, rows,
-    wanted_hbm, place_ref, acc_ref, embedding_ref, state_ref,
+    wanted_hbm, places_ref, relayed_ref, acc_ref, embedding_ref, state_ref,
     table, new_state_ref, next_ref,
-    wanted_ref, picked, outgoing, incoming, place, total, rate_ref, wanted_sem, data_send, data_recv,
+    wanted_ref, picked, outgoing, incoming, relay_in, place, total, partial, summed, rate_ref,
+    wanted_sem, data_send, data_recv, relay_recv, raw_sems,
 ):
     devices = dp * rows
     slots = outgoing.shape[0]
@@ -351,13 +456,35 @@
     update(acc_ref, embedding_ref, state_ref, new_state_ref, rate_ref, table)
     load.wait()
 
-    def copy(dz, dr):
+    inner = is_inner(dp)
+    plane = rows * capacity
+    z, r = lax.axis_index("dp"), lax.axis_index("rows")
+
+    def span_of(i):
+        return pl.ds(pl.multiple_of(i * capacity, capacity), capacity)
+
+    def answer(dz, dr):
         i = dz * rows + dr
-        span = pl.ds(pl.multiple_of(i * capacity, capacity), capacity)
         return pltpu.make_async_remote_copy(
-            src_ref=outgoing.at[span, :], dst_ref=incoming.at[span, :],
+            src_ref=outgoing.at[span_of(i), :], dst_ref=incoming.at[span_of(i), :],
             send_sem=data_send.at[i], recv_sem=data_recv.at[i],
             device_id=peer(dp, rows, dz, dr), device_id_type=MESH,
+        )
+
+    def relay(dr, side):
+        i = (3 - inner) * rows + dr
+        k = side * rows + dr
+        return pltpu.make_async_remote_copy(
+            src_ref=outgoing.at[span_of(i), :], dst_ref=relay_in.at[span_of(k), :],
+            send_sem=data_send.at[i], recv_sem=relay_recv.at[k],
+            device_id=(z + (1 - inner) * (1 - 2 * lax.rem(z, 2)), flip(r, dr, rows)),
+            device_id_type=MESH,
+        )
+
+    def send_raw():
+        return pltpu.make_async_remote_copy(
+            src_ref=summed, dst_ref=partial, send_sem=raw_sems.at[0], recv_sem=raw_sems.at[1],
+            device_id=peer(dp, rows, 2, 0), device_id_type=MESH,
         )
 
     def gather(i):
@@ -366,65 +493,125 @@
             picked[pl.ds(k, 1), :] = table[pl.ds(wanted_ref[start + k], 1), :]
         outgoing[pl.ds(start, capacity), :] = picked[...].astype(jnp.bfloat16)
 
-    for position, dz in enumerate(plane_order(dp)):
+    first, second = 3 - inner, 2 + inner
+    gather(first * rows)
+    gathered(dp, rows)
+    side = 1 - inner
+
+    @pl.loop(1, rows)
+    def _(dr):
+        gather(first * rows + dr)
+        pl.when(dr + side > 1)(lambda: relay(dr - 1, side).start())
+
+    relay(rows - 1, side).start()
+
+    for dz in (second, 1, 0):
         gather(dz * rows)
-        if position == 0:
-            gathered(dp, rows)
 
         @pl.loop(1, rows)
         def _(dr):
             gather(dz * rows + dr)
-            if dz:
-                copy(dz, dr - 1).start()
+            if isinstance(dz, int) and dz == 0:
+                pl.when(dr > 1)(lambda: answer(dz, dr - 1).start())
             else:
-                pl.when(dr > 1)(lambda: copy(dz, dr - 1).start())
-
-        copy(dz, rows - 1).start()
-
-    incoming[0:capacity, :] = outgoing[0:capacity, :]
-    total[...] = jnp.zeros(total.shape, jnp.float32)
-    for b in range(place_ref.shape[0]):
-        row = place_ref[b : b + 1, :].astype(jnp.float32)
-        place[b * LANES : (b + 1) * LANES, :] = jnp.broadcast_to(row, (LANES, LANES)).T.astype(
-            jnp.int32
-        )
+                answer(dz, dr - 1).start()
+
+        answer(dz, rows - 1).start()
 
     lookups = total.shape[0]
     per_plane = rows // group
-    for dz in plane_order(dp):
-
+
+    def turn(source):
+        for b in range(source.shape[0]):
+            row = source[b : b + 1, :].astype(jnp.float32)
+            place[b * LANES : (b + 1) * LANES, :] = jnp.broadcast_to(row, (LANES, LANES)).T.astype(
+                jnp.int32
+            )
+        total[...] = jnp.zeros(total.shape, jnp.float32)
+
+    def put(base, blocks, start):
+        lane = lax.broadcasted_iota(jnp.int32, (lookups, capacity), 1)
+        chosen = jnp.concatenate(
+            [
+                jnp.where(place[:, :capacity] == lane + (base + start + k * capacity), 1.0, 0.0)
+                for k in range(group)
+            ],
+            axis=1,
+        ).astype(jnp.bfloat16)
+        total[...] += jnp.dot(
+            chosen, blocks[pl.ds(start, depth), :], preferred_element_type=jnp.float32
+        )
+
+    @pl.when(inner == 1)
+    def _():
+        relay_in[0:capacity, :] = outgoing[2 * plane : 2 * plane + capacity, :]
+        turn(relayed_ref[1])
+        for half in range(2):
+
+            @pl.loop(0, per_plane)
+            def _(step):
+                for k in range(group):
+                    dr = step * group + k
+
+                    def arrive():
+                        relay(dr, half).wait_recv()
+
+                    if half == 0:
+                        pl.when(dr > 0)(arrive)
+                    else:
+                        arrive()
+                start = half * plane + step * depth
+                put(2 * plane, relay_in, pl.multiple_of(start, depth))
+
+        summed[...] = total[...].astype(jnp.bfloat16)
+
+    turn(places_ref[1])
+
+    @pl.when(inner == 1)
+    def _():
+        send_raw().start()
+
+    incoming[0:capacity, :] = outgoing[0:capacity, :]
+
+    def take_plane(dz):
         @pl.loop(0, per_plane)
         def _(step):
             for k in range(group):
                 dr = step * group + k
 
                 def arrive():
-                    copy(dz, dr).wait_recv()
+                    answer(dz, dr).wait_recv()
 
                 if dz == 0:
                     pl.when(dr > 0)(arrive)
                 else:
                     arrive()
-            start = pl.multiple_of((dz * per_plane + step) * depth, depth)
-            lane = lax.broadcasted_iota(jnp.int32, (lookups, capacity), 1)
-            chosen = jnp.concatenate(
-                [
-                    jnp.where(place[:, :capacity] == lane + (start + k * capacity), 1.0, 0.0)
-                    for k in range(group)
-                ],
-                axis=1,
-            ).astype(jnp.bfloat16)
-            total[...] += jnp.dot(
-                chosen, incoming[pl.ds(start, depth), :], preferred_element_type=jnp.float32
-            )
-
-    next_ref[...] = total[...].astype(jnp.bfloat16)
-
-    for dz in plane_order(dp):
-
-        @pl.loop(0 if dz else 1, rows)
+            put(0, incoming, pl.multiple_of(dz * plane + step * depth, depth))
+
+    take_plane(0)
+    take_plane(1)
+
+    @pl.when(inner == 1)
+    def _():
+        take_plane(2)
+        take_plane(3)
+        next_ref[...] = total[...].astype(jnp.bfloat16)
+        send_raw().wait_send()
+
+    @pl.when(inner == 0)
+    def _():
+        send_raw().wait_recv()
+        next_ref[...] = (total[...] + partial[...].astype(jnp.float32)).astype(jnp.bfloat16)
+
+    @pl.loop(inner, rows)
+    def _(dr):
+        relay(dr, side).wait_send()
+
+    for dz in (second, 1, 0):
+
+        @pl.loop(1 if isinstance(dz, int) and dz == 0 else 0, rows)
         def _(dr):
-            copy(dz, dr).wait_send()
+            answer(dz, dr).wait_send()
 
 
 def finish_kernel(*refs):
@@ -460,10 +647,10 @@
     )(*arrays)
 
 
-def fetch(dp, rows, wanted, place, acc, embedding, state):
+def fetch(dp, rows, wanted, places, relayed, acc, embedding, state):
     slots = wanted.shape[0]
     devices = dp * rows
-    lookups = place.shape[0] * place.shape[1]
+    lookups = places.shape[1] * places.shape[2]
     owned, columns = embedding.shape
     tiles = (owned // LANES, LANES)
     vmem = pl.BlockSpec(memory_space=pltpu.VMEM)
@@ -476,36 +663,41 @@
             jax.ShapeDtypeStruct(tiles, jnp.float32),
             jax.ShapeDtypeStruct((lookups, columns), jnp.bfloat16),
         ),
-        in_specs=[hbm] + [vmem] * 4,
+        in_specs=[hbm] + [vmem] * 5,
         out_specs=(vmem,) * 3,
         scratch_shapes=[
             pltpu.SMEM((slots,), jnp.int32),
             pltpu.VMEM((slots // devices, columns), jnp.float32),
             pltpu.VMEM((slots, columns), jnp.bfloat16),
             pltpu.VMEM((slots, columns), jnp.bfloat16),
+            pltpu.VMEM((slots // 2, columns), jnp.bfloat16),
             pltpu.VMEM((lookups, LANES), jnp.int32),
             pltpu.VMEM((lookups, columns), jnp.float32),
+            pltpu.VMEM((lookups, columns), jnp.bfloat16),
+            pltpu.VMEM((lookups, columns), jnp.bfloat16),
             pltpu.VMEM(tiles, jnp.float32),
             pltpu.SemaphoreType.DMA,
             pltpu.SemaphoreType.DMA((devices,)),
             pltpu.SemaphoreType.DMA((devices,)),
+            pltpu.SemaphoreType.DMA((2 * rows,)),
+            pltpu.SemaphoreType.DMA((2,)),
         ],
         compiler_params=pltpu.CompilerParams(
             collective_id=1, has_side_effects=True, vmem_limit_bytes=40 * 1024 * 1024
         ),
-    )(wanted, place, acc, embedding, state.reshape(tiles))
+    )(wanted, places, relayed, acc, embedding, state.reshape(tiles))
     new_embedding, new_state, next_rows = finish(table, new_state, next_rows)
     return new_embedding, new_state.reshape(owned), next_rows
 
 
 def on_device(owners, offsets, gradients, embedding, adagrad_state, next_owners, next_offsets):
     dp, rows = lax.axis_size("dp"), lax.axis_size("rows")
-    acc, met, next_place = send_gradients(
+    acc, met, places, relayed = send_gradients(
         dp, rows, owners, offsets, next_owners, next_offsets, gradients, embedding.shape[0]
     )
     wanted = met[:, 0, met.shape[2] // 2 :].reshape(-1)
     new_embedding, new_state, next_rows = fetch(
-        dp, rows, wanted, next_place, acc, embedding, adagrad_state
+        dp, rows, wanted, places, relayed, acc, embedding, adagrad_state
     )
     return (new_embedding, new_state, next_rows)
 

time: 76.1 us -> 72.1 us (0.947)
  the two profiles are of different devices: /device:TPU:0 before, /device:TPU:9 now
where the time goes in v5:
time: 72.1 us; the launch traced here: 71.9 us
  Pallas kernels  69.5 us (96%)
  local copies, waits for them, and re-layouts  0.97 us (1%)
  other arithmetic  0.74 us (1%)
    pallas_call x1, Pallas kernels, send_gradients(): pl.pallas_call(functools.partial(send_kernel, dp, rows), name='send_gradi...  37.9 us
    pallas_call x1, Pallas kernels, fetch(): pl.pallas_call(functools.partial(fetch_kernel, dp, rows), name='fetch', o...  29.4 us
    pallas_call x1, Pallas kernels, finish(): pl.pallas_call(finish_kernel, name='finish', out_shape=tuple((jax.ShapeDt...  2.19 us

profile of v5, /device:TPU:9, one launch (start us, length us, event | category | flops | bytes accessed | tf_op | source)
XLA Modules:
  0.0 71.9 jit_solution(18385906668303551482)
XLA Ops:
  0.6 0.7 %pad_add_fusion.index_ref = s32[4,8,128]{2,1,0:T(8,128)S(1)} fusion(s32[1,8,128]{2,1,0:T(8,128)} %bitcast.9, s32[1,8,128]{2,1,0:T(8,128)} %bitcast.10, s32[1,8,128]{2,1,0:T(8,128)} %bitcast.11, s32[1,8,128]{2,1,0:T(8,128)} %bitcast.12), kind=kLoop, calls=%fused_computation | loop fusion | flops 12288 | bytes 32768 | tf_op jit(solution)/shard_map/stack | solution.py:376
  1.4 0.0 copy-start.2
  1.4 0.9 %copy-done.2 = bf16[1024,128]{1,0:T(8,128)(2,1)S(1)} copy-done((bf16[1024,128]{1,0:T(8,128)(2,1)S(1)}, bf16[1024,128]{1,0:T(8,128)(2,1)}, u32[]{:S(2)}) %copy-start.2) | copy-done | bytes 262168
  2.3 0.0 copy-start
  2.3 0.0 copy-start.1
  2.3 37.9 %send_gradients.1 = (f32[4096,256]{1,0:T(8,128)S(1)}, s32[32,1,256]{2,1,0:T(1,128)S(1)}, s32[2,8,128]{2,1,0:T(8,128)S(1)}, s32[2,8,128]{2,1,0:T(8,128)S(1)}) custom-call(s32[4,8,128]{2,1,0:T(8,128)S(1)} %pad_add_fusion.index_ref, bf16[1024,128]{1,0:T(8,128)(2,1)S(1)} %copy-done.2), custom_call_target="tpu_custom_call" | custom-call | flops 1717986918400 | bytes 4194304 | tf_op jit(solution)/shard_map/send_gradients/pallas_call | solution.py:348
  40.3 0.0 copy-done
  40.3 0.0 copy-done.1
  40.3 29.4 %fetch.1 = (f32[8192,128]{1,0:T(8,128)S(1)}, f32[64,128]{1,0:T(8,128)S(1)}, bf16[1024,128]{1,0:T(8,128)(2,1)S(1)}) custom-call(s32[4096]{0:T(1024)S(1)} %bitcast.7, s32[2,8,128]{2,1,0:T(8,128)S(1)} %get-tuple-element.14.places_ref, s32[2,8,128]{2,1,0:T(8,128)S(1)} %get-tuple-element.15.relayed_ref, f32[4096,256]{1,0:T(8,128)S(1)} %get-tuple-element.16.acc_ref, ...), custom_call_target="tpu_custom_call" | custom-call | tf_op jit(solution)/shard_map/fetch/pallas_call | solution.py:658
  69.7 2.2 %finish.1 = (f32[8192,128]{1,0:T(8,128)}, f32[64,128]{1,0:T(8,128)}, bf16[1024,128]{1,0:T(8,128)(2,1)}) custom-call(f32[8192,128]{1,0:T(8,128)S(1)} %get-tuple-element.17.refs_0_, f32[64,128]{1,0:T(8,128)S(1)} %get-tuple-element.18.refs_1_, bf16[1024,128]{1,0:T(8,128)(2,1)S(1)} %get-tuple-element.19.refs_2_), custom_call_target="tpu_custom_call" | custom-call | tf_op jit(solution)/shard_map/finish/pallas_call | solution.py:639
  (1 shorter events, 0.0 us)
Async XLA Ops:
  1.4 0.9 %copy-start.2 = (bf16[1024,128]{1,0:T(8,128)(2,1)S(1)}, bf16[1024,128]{1,0:T(8,128)(2,1)}, u32[]{:S(2)}) copy-start(bf16[1024,128]{1,0:T(8,128)(2,1)} %gradients_ref.1) | copy-start | bytes 786436
  2.3 37.9 %copy-start = (f32[8192,128]{1,0:T(8,128)S(1)}, f32[8192,128]{1,0:T(8,128)}, u32[]{:S(2)}) copy-start(f32[8192,128]{1,0:T(8,128)} %embedding_ref.1) | copy-start | bytes 12582916
  2.3 37.9 %copy-start.1 = (f32[8192]{0:T(1024)S(1)}, f32[8192]{0:T(1024)}, u32[]{:S(2)}) copy-start(f32[8192]{0:T(1024)} %param.11) | copy-start | bytes 98308

commit v6 on v5

--- a/solution.py
+++ b/solution.py
@@ -199,11 +199,7 @@
         )
 
     pick = builder(place)
-
-    @pl.when(inner == 1)
-    def _():
-        build(pick, gradients_ref, outgoing, 2, 0)
-
+    build(pick, gradients_ref, outgoing, 1, 0)
     gathered(dp, rows)
 
     @pl.when(inner == 0)
@@ -219,20 +215,15 @@
         for dr in range(0 if dz else 1, rows):
             send_data(dz, dr).start()
 
-    @pl.when(inner == 1)
-    def _():
-        send_plane(2)
-
-    build(pick, gradients_ref, outgoing, 1, 0)
     send_plane(1)
-
-    @pl.when(inner == 1)
-    def _():
-        build(pick, gradients_ref, outgoing, 3, 0)
-        send_plane(3)
-
     build(pick, gradients_ref, outgoing, 0, 0)
     send_plane(0)
+
+    @pl.when(inner == 1)
+    def _():
+        for dz in (2, 3):
+            build(pick, gradients_ref, outgoing, dz, 0)
+            send_plane(dz)
 
     @pl.loop(0, half // LANES)
     def _(step):
@@ -243,7 +234,7 @@
     met_ref[0] = meta_ref[0]
     incoming[0:capacity, :] = outgoing[0:capacity, :]
 
-    chunk = min(1024, half)
+    chunk = min(4096, half)
 
     def accumulate(tile):
         met = [met_ref[tile * group + k][:, :capacity] for k in range(group)]
@@ -296,7 +287,6 @@
             accumulate(dz * per_plane + step)
 
     take_plane(0)
-    take_plane(1)
 
     @pl.when(inner == 1)
     def _():
@@ -309,6 +299,7 @@
                 relay_data(dz, dr).start()
         incoming[2 * plane : 2 * plane + capacity, :] = relay_out[0:capacity, :]
 
+    take_plane(1)
     take_plane(2)
     take_plane(3)
 
@@ -393,7 +384,7 @@
     ones = jnp.ones((2 * LANES, LANES), jnp.bfloat16)
     sides = table.shape[0] // half
 
-    batch = min(8, tiles)
+    batch = min(16, tiles)
 
     for side in range(sides):
 
@@ -498,25 +489,22 @@
     gathered(dp, rows)
     side = 1 - inner
 
-    @pl.loop(1, rows)
-    def _(dr):
+    for dr in range(1, rows):
         gather(first * rows + dr)
-        pl.when(dr + side > 1)(lambda: relay(dr - 1, side).start())
-
+        if dr == 1:
+            pl.when(inner == 0)(lambda: relay(0, side).start())
+        else:
+            relay(dr - 1, side).start()
     relay(rows - 1, side).start()
 
     for dz in (second, 1, 0):
-        gather(dz * rows)
-
-        @pl.loop(1, rows)
+
+        @pl.loop(0, rows)
         def _(dr):
             gather(dz * rows + dr)
-            if isinstance(dz, int) and dz == 0:
-                pl.when(dr > 1)(lambda: answer(dz, dr - 1).start())
-            else:
-                answer(dz, dr - 1).start()
-
-        answer(dz, rows - 1).start()
+
+        for dr in range(1 if isinstance(dz, int) and dz == 0 else 0, rows):
+            answer(dz, dr).start()
 
     lookups = total.shape[0]
     per_plane = rows // group

time: 72.1 us -> 62 us (0.86)
  Pallas kernels: 69.5 us -> 59.4 us
    pallas_call x1, Pallas kernels: 37.9 us -> 28.7 us  [send_gradients(): pl.pallas_call(functools.partial(send_kernel, dp, rows), name='send_gradi...]
    pallas_call x1, Pallas kernels: 29.4 us -> 28.5 us  [fetch(): pl.pallas_call(functools.partial(fetch_kernel, dp, rows), name='fetch', o...]
where the time goes in v6:
time: 62 us; the launch traced here: 61.8 us
  Pallas kernels  59.4 us (96%)
  local copies, waits for them, and re-layouts  0.97 us (2%)
  other arithmetic  0.74 us (1%)
  between operations  0.67 us (1%)
    pallas_call x1, Pallas kernels, send_gradients(): pl.pallas_call(functools.partial(send_kernel, dp, rows), name='send_gradi...  28.7 us
    pallas_call x1, Pallas kernels, fetch(): pl.pallas_call(functools.partial(fetch_kernel, dp, rows), name='fetch', o...  28.5 us
    pallas_call x1, Pallas kernels, finish(): pl.pallas_call(finish_kernel, name='finish', out_shape=tuple((jax.ShapeDt...  2.19 us

profile of v6, /device:TPU:9, one launch (start us, length us, event | category | flops | bytes accessed | tf_op | source)
XLA Modules:
  0.0 61.8 jit_solution(11651548902135706935)
XLA Ops:
  0.6 0.7 %pad_add_fusion.index_ref = s32[4,8,128]{2,1,0:T(8,128)S(1)} fusion(s32[1,8,128]{2,1,0:T(8,128)} %bitcast.9, s32[1,8,128]{2,1,0:T(8,128)} %bitcast.10, s32[1,8,128]{2,1,0:T(8,128)} %bitcast.11, s32[1,8,128]{2,1,0:T(8,128)} %bitcast.12), kind=kLoop, calls=%fused_computation | loop fusion | flops 12288 | bytes 32768 | tf_op jit(solution)/shard_map/stack | solution.py:367
  1.4 0.0 copy-start.2
  1.4 0.9 %copy-done.2 = bf16[1024,128]{1,0:T(8,128)(2,1)S(1)} copy-done((bf16[1024,128]{1,0:T(8,128)(2,1)S(1)}, bf16[1024,128]{1,0:T(8,128)(2,1)}, u32[]{:S(2)}) %copy-start.2) | copy-done | bytes 262168
  2.3 0.0 copy-start
  2.3 0.0 copy-start.1
  2.3 28.7 %send_gradients.1 = (f32[4096,256]{1,0:T(8,128)S(1)}, s32[32,1,256]{2,1,0:T(1,128)S(1)}, s32[2,8,128]{2,1,0:T(8,128)S(1)}, s32[2,8,128]{2,1,0:T(8,128)S(1)}) custom-call(s32[4,8,128]{2,1,0:T(8,128)S(1)} %pad_add_fusion.index_ref, bf16[1024,128]{1,0:T(8,128)(2,1)S(1)} %copy-done.2), custom_call_target="tpu_custom_call" | custom-call | flops 1717986918400 | bytes 4194304 | tf_op jit(solution)/shard_map/send_gradients/pallas_call | solution.py:339
  31.1 0.0 copy-done
  31.1 0.0 copy-done.1
  31.1 28.5 %fetch.1 = (f32[8192,128]{1,0:T(8,128)S(1)}, f32[64,128]{1,0:T(8,128)S(1)}, bf16[1024,128]{1,0:T(8,128)(2,1)S(1)}) custom-call(s32[4096]{0:T(1024)S(1)} %bitcast.7, s32[2,8,128]{2,1,0:T(8,128)S(1)} %get-tuple-element.14.places_ref, s32[2,8,128]{2,1,0:T(8,128)S(1)} %get-tuple-element.15.relayed_ref, f32[4096,256]{1,0:T(8,128)S(1)} %get-tuple-element.16.acc_ref, ...), custom_call_target="tpu_custom_call" | custom-call | tf_op jit(solution)/shard_map/fetch/pallas_call | solution.py:646
  59.6 2.2 %finish.1 = (f32[8192,128]{1,0:T(8,128)}, f32[64,128]{1,0:T(8,128)}, bf16[1024,128]{1,0:T(8,128)(2,1)}) custom-call(f32[8192,128]{1,0:T(8,128)S(1)} %get-tuple-element.17.refs_0_, f32[64,128]{1,0:T(8,128)S(1)} %get-tuple-element.18.refs_1_, bf16[1024,128]{1,0:T(8,128)(2,1)S(1)} %get-tuple-element.19.refs_2_), custom_call_target="tpu_custom_call" | custom-call | tf_op jit(solution)/shard_map/finish/pallas_call | solution.py:627
  (1 shorter events, 0.0 us)
Async XLA Ops:
  1.4 0.9 %copy-start.2 = (bf16[1024,128]{1,0:T(8,128)(2,1)S(1)}, bf16[1024,128]{1,0:T(8,128)(2,1)}, u32[]{:S(2)}) copy-start(bf16[1024,128]{1,0:T(8,128)(2,1)} %gradients_ref.1) | copy-start | bytes 786436
  2.3 28.7 %copy-start = (f32[8192,128]{1,0:T(8,128)S(1)}, f32[8192,128]{1,0:T(8,128)}, u32[]{:S(2)}) copy-start(f32[8192,128]{1,0:T(8,128)} %embedding_ref.1) | copy-start | bytes 12582916
  2.3 28.8 %copy-start.1 = (f32[8192]{0:T(1024)S(1)}, f32[8192]{0:T(1024)}, u32[]{:S(2)}) copy-start(f32[8192]{0:T(1024)} %param.11) | copy-start | bytes 98308

commit v7 on v6

--- a/solution.py
+++ b/solution.py
@@ -384,7 +384,7 @@
     ones = jnp.ones((2 * LANES, LANES), jnp.bfloat16)
     sides = table.shape[0] // half
 
-    batch = min(16, tiles)
+    batch = min(32, tiles)
 
     for side in range(sides):
 
@@ -438,7 +438,7 @@
     devices = dp * rows
     slots = outgoing.shape[0]
     capacity = slots // devices
-    group = 2 if capacity == LANES else 1
+    group = 4 if capacity == LANES else 1
     depth = group * capacity
 
     greet(dp, rows)
@@ -553,13 +553,13 @@
 
         summed[...] = total[...].astype(jnp.bfloat16)
 
+    incoming[0:capacity, :] = outgoing[0:capacity, :]
+
+    @pl.when(inner == 1)
+    def _():
+        send_raw().start()
+
     turn(places_ref[1])
-
-    @pl.when(inner == 1)
-    def _():
-        send_raw().start()
-
-    incoming[0:capacity, :] = outgoing[0:capacity, :]
 
     def take_plane(dz):
         @pl.loop(0, per_plane)

time: 62 us -> 60.7 us (0.979)
  Pallas kernels: 59.4 us -> 58.1 us
    pallas_call x1, Pallas kernels: 28.5 us -> 27.2 us  [fetch(): pl.pallas_call(functools.partial(fetch_kernel, dp, rows), name='fetch', o...]
where the time goes in v7:
time: 60.7 us; the launch traced here: 60.5 us
  Pallas kernels  58.1 us (96%)
  local copies, waits for them, and re-layouts  0.97 us (2%)
  other arithmetic  0.74 us (1%)
  between operations  0.67 us (1%)
    pallas_call x1, Pallas kernels, send_gradients(): pl.pallas_call(functools.partial(send_kernel, dp, rows), name='send_gradi...  28.7 us
    pallas_call x1, Pallas kernels, fetch(): pl.pallas_call(functools.partial(fetch_kernel, dp, rows), name='fetch', o...  27.2 us
    pallas_call x1, Pallas kernels, finish(): pl.pallas_call(finish_kernel, name='finish', out_shape=tuple((jax.ShapeDt...  2.19 us

profile of v7, /device:TPU:9, one launch (start us, length us, event | category | flops | bytes accessed | tf_op | source)
XLA Modules:
  0.0 60.5 jit_solution(11579174276949115958)
XLA Ops:
  0.6 0.7 %pad_add_fusion.index_ref = s32[4,8,128]{2,1,0:T(8,128)S(1)} fusion(s32[1,8,128]{2,1,0:T(8,128)} %bitcast.9, s32[1,8,128]{2,1,0:T(8,128)} %bitcast.10, s32[1,8,128]{2,1,0:T(8,128)} %bitcast.11, s32[1,8,128]{2,1,0:T(8,128)} %bitcast.12), kind=kLoop, calls=%fused_computation | loop fusion | flops 12288 | bytes 32768 | tf_op jit(solution)/shard_map/stack | solution.py:367
  1.4 0.0 copy-start.2
  1.4 0.9 %copy-done.2 = bf16[1024,128]{1,0:T(8,128)(2,1)S(1)} copy-done((bf16[1024,128]{1,0:T(8,128)(2,1)S(1)}, bf16[1024,128]{1,0:T(8,128)(2,1)}, u32[]{:S(2)}) %copy-start.2) | copy-done | bytes 262168
  2.3 0.0 copy-start
  2.3 0.0 copy-start.1
  2.3 28.7 %send_gradients.1 = (f32[4096,256]{1,0:T(8,128)S(1)}, s32[32,1,256]{2,1,0:T(1,128)S(1)}, s32[2,8,128]{2,1,0:T(8,128)S(1)}, s32[2,8,128]{2,1,0:T(8,128)S(1)}) custom-call(s32[4,8,128]{2,1,0:T(8,128)S(1)} %pad_add_fusion.index_ref, bf16[1024,128]{1,0:T(8,128)(2,1)S(1)} %copy-done.2), custom_call_target="tpu_custom_call" | custom-call | flops 1717986918400 | bytes 4194304 | tf_op jit(solution)/shard_map/send_gradients/pallas_call | solution.py:339
  31.1 0.0 copy-done
  31.1 0.0 copy-done.1
  31.1 27.2 %fetch.1 = (f32[8192,128]{1,0:T(8,128)S(1)}, f32[64,128]{1,0:T(8,128)S(1)}, bf16[1024,128]{1,0:T(8,128)(2,1)S(1)}) custom-call(s32[4096]{0:T(1024)S(1)} %bitcast.7, s32[2,8,128]{2,1,0:T(8,128)S(1)} %get-tuple-element.14.places_ref, s32[2,8,128]{2,1,0:T(8,128)S(1)} %get-tuple-element.15.relayed_ref, f32[4096,256]{1,0:T(8,128)S(1)} %get-tuple-element.16.acc_ref, ...), custom_call_target="tpu_custom_call" | custom-call | tf_op jit(solution)/shard_map/fetch/pallas_call | solution.py:646
  58.3 2.2 %finish.1 = (f32[8192,128]{1,0:T(8,128)}, f32[64,128]{1,0:T(8,128)}, bf16[1024,128]{1,0:T(8,128)(2,1)}) custom-call(f32[8192,128]{1,0:T(8,128)S(1)} %get-tuple-element.17.refs_0_, f32[64,128]{1,0:T(8,128)S(1)} %get-tuple-element.18.refs_1_, bf16[1024,128]{1,0:T(8,128)(2,1)S(1)} %get-tuple-element.19.refs_2_), custom_call_target="tpu_custom_call" | custom-call | tf_op jit(solution)/shard_map/finish/pallas_call | solution.py:627
  (1 shorter events, 0.0 us)
Async XLA Ops:
  1.4 0.9 %copy-start.2 = (bf16[1024,128]{1,0:T(8,128)(2,1)S(1)}, bf16[1024,128]{1,0:T(8,128)(2,1)}, u32[]{:S(2)}) copy-start(bf16[1024,128]{1,0:T(8,128)(2,1)} %gradients_ref.1) | copy-start | bytes 786436
  2.3 28.7 %copy-start = (f32[8192,128]{1,0:T(8,128)S(1)}, f32[8192,128]{1,0:T(8,128)}, u32[]{:S(2)}) copy-start(f32[8192,128]{1,0:T(8,128)} %embedding_ref.1) | copy-start | bytes 12582916
  2.3 28.8 %copy-start.1 = (f32[8192]{0:T(1024)S(1)}, f32[8192]{0:T(1024)}, u32[]{:S(2)}) copy-start(f32[8192]{0:T(1024)} %param.11) | copy-start | bytes 98308

commit v8 on v7

--- a/solution.py
+++ b/solution.py
@@ -301,7 +301,6 @@
 
     take_plane(1)
     take_plane(2)
-    take_plane(3)
 
     for dz in range(dp):
 
@@ -310,6 +309,8 @@
             send_meta(dz, dr).wait_send()
             if dz < 2:
                 send_data(dz, dr).wait_send()
+
+    take_plane(3)
 
     @pl.when(inner == 1)
     def _():
@@ -579,6 +580,10 @@
     take_plane(0)
     take_plane(1)
 
+    @pl.loop(inner, rows)
+    def _(dr):
+        relay(dr, side).wait_send()
+
     @pl.when(inner == 1)
     def _():
         take_plane(2)
@@ -590,10 +595,6 @@
     def _():
         send_raw().wait_recv()
         next_ref[...] = (total[...] + partial[...].astype(jnp.float32)).astype(jnp.bfloat16)
-
-    @pl.loop(inner, rows)
-    def _(dr):
-        relay(dr, side).wait_send()
 
     for dz in (second, 1, 0):
 

time: 60.7 us -> 60.4 us (level)
  no operation moved by 1% of the time
where the time goes in v8:
time: 60.4 us; the launch traced here: 60.2 us
  Pallas kernels  57.8 us (96%)
  local copies, waits for them, and re-layouts  0.97 us (2%)
  other arithmetic  0.74 us (1%)
  between operations  0.67 us (1%)
    pallas_call x1, Pallas kernels, send_gradients(): pl.pallas_call(functools.partial(send_kernel, dp, rows), name='send_gradi...  28.7 us
    pallas_call x1, Pallas kernels, fetch(): pl.pallas_call(functools.partial(fetch_kernel, dp, rows), name='fetch', o...  26.9 us
    pallas_call x1, Pallas kernels, finish(): pl.pallas_call(finish_kernel, name='finish', out_shape=tuple((jax.ShapeDt...  2.19 us

profile of v8, /device:TPU:9, one launch (start us, length us, event | category | flops | bytes accessed | tf_op | source)
XLA Modules:
  0.0 60.2 jit_solution(16100199079580331195)
XLA Ops:
  0.6 0.7 %pad_add_fusion.index_ref = s32[4,8,128]{2,1,0:T(8,128)S(1)} fusion(s32[1,8,128]{2,1,0:T(8,128)} %bitcast.9, s32[1,8,128]{2,1,0:T(8,128)} %bitcast.10, s32[1,8,128]{2,1,0:T(8,128)} %bitcast.11, s32[1,8,128]{2,1,0:T(8,128)} %bitcast.12), kind=kLoop, calls=%fused_computation | loop fusion | flops 12288 | bytes 32768 | tf_op jit(solution)/shard_map/stack | solution.py:368
  1.4 0.0 copy-start.2
  1.4 0.9 %copy-done.2 = bf16[1024,128]{1,0:T(8,128)(2,1)S(1)} copy-done((bf16[1024,128]{1,0:T(8,128)(2,1)S(1)}, bf16[1024,128]{1,0:T(8,128)(2,1)}, u32[]{:S(2)}) %copy-start.2) | copy-done | bytes 262168
  2.3 0.0 copy-start
  2.3 0.0 copy-start.1
  2.3 28.7 %send_gradients.1 = (f32[4096,256]{1,0:T(8,128)S(1)}, s32[32,1,256]{2,1,0:T(1,128)S(1)}, s32[2,8,128]{2,1,0:T(8,128)S(1)}, s32[2,8,128]{2,1,0:T(8,128)S(1)}) custom-call(s32[4,8,128]{2,1,0:T(8,128)S(1)} %pad_add_fusion.index_ref, bf16[1024,128]{1,0:T(8,128)(2,1)S(1)} %copy-done.2), custom_call_target="tpu_custom_call" | custom-call | flops 1717986918400 | bytes 4194304 | tf_op jit(solution)/shard_map/send_gradients/pallas_call | solution.py:340
  31.1 0.0 copy-done
  31.1 0.0 copy-done.1
  31.1 26.9 %fetch.1 = (f32[8192,128]{1,0:T(8,128)S(1)}, f32[64,128]{1,0:T(8,128)S(1)}, bf16[1024,128]{1,0:T(8,128)(2,1)S(1)}) custom-call(s32[4096]{0:T(1024)S(1)} %bitcast.7, s32[2,8,128]{2,1,0:T(8,128)S(1)} %get-tuple-element.14.places_ref, s32[2,8,128]{2,1,0:T(8,128)S(1)} %get-tuple-element.15.relayed_ref, f32[4096,256]{1,0:T(8,128)S(1)} %get-tuple-element.16.acc_ref, ...), custom_call_target="tpu_custom_call" | custom-call | tf_op jit(solution)/shard_map/fetch/pallas_call | solution.py:647
  58.0 2.2 %finish.1 = (f32[8192,128]{1,0:T(8,128)}, f32[64,128]{1,0:T(8,128)}, bf16[1024,128]{1,0:T(8,128)(2,1)}) custom-call(f32[8192,128]{1,0:T(8,128)S(1)} %get-tuple-element.17.refs_0_, f32[64,128]{1,0:T(8,128)S(1)} %get-tuple-element.18.refs_1_, bf16[1024,128]{1,0:T(8,128)(2,1)S(1)} %get-tuple-element.19.refs_2_), custom_call_target="tpu_custom_call" | custom-call | tf_op jit(solution)/shard_map/finish/pallas_call | solution.py:628
  (1 shorter events, 0.0 us)
Async XLA Ops:
  1.4 0.9 %copy-start.2 = (bf16[1024,128]{1,0:T(8,128)(2,1)S(1)}, bf16[1024,128]{1,0:T(8,128)(2,1)}, u32[]{:S(2)}) copy-start(bf16[1024,128]{1,0:T(8,128)(2,1)} %gradients_ref.1) | copy-start | bytes 786436
  2.3 28.8 %copy-start = (f32[8192,128]{1,0:T(8,128)S(1)}, f32[8192,128]{1,0:T(8,128)}, u32[]{:S(2)}) copy-start(f32[8192,128]{1,0:T(8,128)} %embedding_ref.1) | copy-start | bytes 12582916
  2.3 28.8 %copy-start.1 = (f32[8192]{0:T(1024)S(1)}, f32[8192]{0:T(1024)}, u32[]{:S(2)}) copy-start(f32[8192]{0:T(1024)} %param.11) | copy-start | bytes 98308
